TPU v7x, 32 devices: a whole 2x2x4 slice. The times are simulated.
32 devices in a mesh: clip: 4 (over z), seq: 4 (over x, core), head: 2 (over y).
Axes of the slice: x: 2, y: 2, z: 4, core: 2. Of those that a mesh axis runs over, the one named last changes fastest.
Arguments:
- inputs: float32 [4, 16, 196, 768], P('clip', 'seq'), may hold values from -39 to 39, as said below
- space_gain: float32 [768], P(('clip', 'seq')), may hold values from 0.5 to 1.5
- space_shift: float32 [768], P(('clip', 'seq')), may hold values from -3 to 3
- space_proj: float32 [768, 3, 768], P(('clip', 'seq'), None, 'head'), may hold values from -0.3125 to 0.3125
- space_bias: float32 [2, 6, 128], P(None, 'head', ('clip', 'seq')), may hold values from -3 to 3
- space_out: float32 [768, 768], P('head', ('clip', 'seq')), may hold values from -0.875 to 0.875
- space_out_bias: float32 [768], P(('clip', 'seq')), may hold values from -3 to 3
- time_gain: float32 [768], P(('clip', 'seq')), may hold values from 0.5 to 1.5
- time_shift: float32 [768], P(('clip', 'seq')), may hold values from -3 to 3
- time_proj: float32 [768, 3, 768], P(('clip', 'seq'), None, 'head'), may hold values from -0.3125 to 0.3125
- time_bias: float32 [2, 6, 128], P(None, 'head', ('clip', 'seq')), may hold values from -3 to 3
- time_out: float32 [768, 768], P('head', ('clip', 'seq')), may hold values from -0.4375 to 0.4375
- time_out_bias: float32 [768], P(('clip', 'seq')), may hold values from -3 to 3
- dense_gain: float32 [768], P(('clip', 'seq')), may hold values from 0.5 to 1.5
- dense_shift: float32 [768], P(('clip', 'seq')), may hold values from -3 to 3
- dense_in: float32 [768, 3072], P(('clip', 'seq'), 'head'), may hold values from -0.21875 to 0.21875
- dense_bias: float32 [24, 128], P('head', ('clip', 'seq')), may hold values from -3 to 3
- dense_out: float32 [3072, 768], P('head', ('clip', 'seq')), may hold values from -0.15625 to 0.15625
- dense_out_bias: float32 [768], P(('clip', 'seq')), may hold values from -3 to 3
- cotangent: float32 [4, 16, 196, 768], P('clip', 'seq'), may hold values from -6 to 6
Outputs:
- outputs: float32 [4, 16, 196, 768], P('clip', 'seq')
- input_grad: float32 [4, 16, 196, 768], P('clip', 'seq')
- grad_space_gain: float32 [768], P(('clip', 'seq'))
- grad_space_shift: float32 [768], P(('clip', 'seq'))
- grad_space_proj: float32 [768, 3, 768], P(('clip', 'seq'), None, 'head')
- grad_space_bias: float32 [2, 6, 128], P(None, 'head', ('clip', 'seq'))
- grad_space_out: float32 [768, 768], P('head', ('clip', 'seq'))
- grad_space_out_bias: float32 [768], P(('clip', 'seq'))
- grad_time_gain: float32 [768], P(('clip', 'seq'))
- grad_time_shift: float32 [768], P(('clip', 'seq'))
- grad_time_proj: float32 [768, 3, 768], P(('clip', 'seq'), None, 'head')
- grad_time_bias: float32 [2, 6, 128], P(None, 'head', ('clip', 'seq'))
- grad_time_out: float32 [768, 768], P('head', ('clip', 'seq'))
- grad_time_out_bias: float32 [768], P(('clip', 'seq'))
- grad_dense_gain: float32 [768], P(('clip', 'seq'))
- grad_dense_shift: float32 [768], P(('clip', 'seq'))
- grad_dense_in: float32 [768, 3072], P(('clip', 'seq'), 'head')
- grad_dense_bias: float32 [24, 128], P('head', ('clip', 'seq'))
- grad_dense_out: float32 [3072, 768], P('head', ('clip', 'seq'))
- grad_dense_out_bias: float32 [768], P(('clip', 'seq'))
Inputs may be any that keep to these rules, and one draw needn't show every extreme that they name: `inputs`: real token features.
All inputs are finite; a program needn't handle non-finite values.
Results may differ from a plain program's by a relative error of at most 0.029.
Values may be sent and summed in bfloat16 or wider, within the bound.
A program may use at most 128 MiB of HBM per device.

v0:
```python
import jax
import jax.numpy as jnp
from jax import lax
from jax.sharding import PartitionSpec as P

HEAD_DIM = 64


norm_eps = 1e-06
ACROSS_PLACES = ("cfphe", "cfqhe", "cfhpq")
ACROSS_FRAMES = ("cfphe", "cgphe", "cphfg")


def product(form, left, right):
    return jnp.einsum(form, left, right, preferred_element_type=jnp.float32)


def layer_norm(values, norm_gain, norm_shift):
    row_mean = jnp.mean(values, axis=-1, keepdims=True)
    centred = values - row_mean
    spread = jnp.mean(centred * centred, axis=-1, keepdims=True)
    return centred * lax.rsqrt(spread + norm_eps) * norm_gain + norm_shift


def norm_back(stream, norm_gain, norm_shift, grad_normed):
    outcome, pullback = jax.vjp(
        layer_norm, stream, norm_gain.astype(jnp.float32), norm_shift.astype(jnp.float32)
    )
    return pullback(grad_normed)


def split_heads(merged_rows):
    local_width = merged_rows.shape[-1] // 3
    shaped = merged_rows.reshape(merged_rows.shape[:-1] + (3, local_width // HEAD_DIM, HEAD_DIM))
    return (shaped[..., 0, :, :], shaped[..., 1, :, :], shaped[..., 2, :, :])


def attend(merged_rows, letters):
    queries, key_rows, value_rows = split_heads(merged_rows)
    query_form, key_form, score_form = letters
    score_scale = HEAD_DIM ** (-0.5)
    scores = (
        product(query_form + "," + key_form + "->" + score_form, queries, key_rows) * score_scale
    )
    highest = jnp.max(scores, axis=-1, keepdims=True)
    weights = jnp.exp(scores - highest)
    totals = jnp.sum(weights, axis=-1, keepdims=True)
    attn_probs = (weights / totals).astype(jnp.bfloat16)
    mixed_rows = product(
        score_form + "," + key_form + "->" + query_form, attn_probs, value_rows
    ).astype(jnp.bfloat16)
    return (mixed_rows.reshape(mixed_rows.shape[:-2] + (-1,)), highest + jnp.log(totals))


def attend_back(merged_rows, log_total, grad_mixed, letters):
    queries, key_rows, value_rows = split_heads(merged_rows)
    query_form, key_form, score_form = letters
    score_scale = HEAD_DIM ** (-0.5)
    to_scores = query_form + "," + key_form + "->" + score_form
    scores = product(to_scores, queries, key_rows) * score_scale
    attn_probs = jnp.exp(scores - log_total)
    grad_heads = grad_mixed.reshape(queries.shape)
    grad_values = product(
        score_form + "," + query_form + "->" + key_form, attn_probs.astype(jnp.bfloat16), grad_heads
    )
    grad_probs = product(to_scores, grad_heads, value_rows)
    grad_scores = attn_probs * (
        grad_probs - jnp.sum(attn_probs * grad_probs, axis=-1, keepdims=True)
    )
    grad_scores = grad_scores.astype(jnp.bfloat16)
    grad_queries = (
        product(score_form + "," + key_form + "->" + query_form, grad_scores, key_rows)
        * score_scale
    )
    grad_keys = (
        product(score_form + "," + query_form + "->" + key_form, grad_scores, queries) * score_scale
    )
    stacked = jnp.stack([grad_queries, grad_keys, grad_values], axis=-3).astype(jnp.bfloat16)
    return stacked.reshape(merged_rows.shape)


def head_total(partial_rows):
    return lax.psum(partial_rows.astype(jnp.bfloat16), "head").astype(jnp.float32)


def project_in(normed_low, proj_local, bias_local):
    model_width = proj_local.shape[0]
    local_width = proj_local.shape[2]
    flat_rows = jnp.dot(
        normed_low.reshape(-1, model_width),
        proj_local.reshape(model_width, 3 * local_width),
        preferred_element_type=jnp.float32,
    )
    bias_rows = bias_local.reshape(2, local_width).astype(jnp.float32)
    bias_full = jnp.concatenate(
        [bias_rows[0:1], jnp.zeros((1, local_width), jnp.float32), bias_rows[1:2]], axis=0
    )
    merged_rows = (flat_rows + bias_full.reshape(1, 3 * local_width)).astype(jnp.bfloat16)
    return merged_rows.reshape(normed_low.shape[:-1] + (3 * local_width,))


def project_out(mixed_rows, out_local, out_bias):
    lead_shape = mixed_rows.shape[:-1]
    partial_rows = jnp.dot(
        mixed_rows.reshape(-1, mixed_rows.shape[-1]), out_local, preferred_element_type=jnp.float32
    )
    summed = head_total(partial_rows)
    return (summed + out_bias.astype(jnp.float32)).reshape(lead_shape + (out_local.shape[1],))


def out_back(grad_stream, mixed_rows, out_local):
    model_width = out_local.shape[1]
    grad_flat = grad_stream.reshape(-1, model_width)
    bias_grad = jnp.sum(grad_flat, axis=0)
    grad_low = grad_flat.astype(jnp.bfloat16)
    mixed_flat = mixed_rows.reshape(-1, mixed_rows.shape[-1])
    weight_grad = product("nw,nd->wd", mixed_flat, grad_low)
    grad_mixed = product("nd,wd->nw", grad_low, out_local).astype(jnp.bfloat16)
    return (bias_grad, weight_grad, grad_mixed.reshape(mixed_rows.shape))


def in_back(grad_merged, normed_low, proj_local, bias_shape):
    model_width = proj_local.shape[0]
    local_width = proj_local.shape[2]
    merged_flat = grad_merged.reshape(-1, 3 * local_width)
    normed_flat = normed_low.reshape(-1, model_width)
    proj_grad = product("nd,nk->dk", normed_flat, merged_flat).reshape(proj_local.shape)
    slot_sums = jnp.sum(merged_flat, axis=0, dtype=jnp.float32).reshape(3, local_width)
    bias_grad = jnp.stack([slot_sums[0], slot_sums[2]]).reshape(bias_shape)
    grad_normed = head_total(
        product("nk,dk->nd", merged_flat, proj_local.reshape(model_width, 3 * local_width))
    )
    return (proj_grad, bias_grad, grad_normed.reshape(normed_low.shape))


def to_places(rows):
    return lax.all_to_all(
        rows.astype(jnp.bfloat16), "seq", split_axis=2, concat_axis=1, tiled=True
    ).astype(rows.dtype)


def to_frames(rows):
    return lax.all_to_all(
        rows.astype(jnp.bfloat16), "seq", split_axis=1, concat_axis=2, tiled=True
    ).astype(rows.dtype)


def gather_forward(lowered):
    return (
        lax.all_gather(lowered[0], ("clip", "seq"), axis=0, tiled=True),
        lax.all_gather(lowered[1], ("clip", "seq"), axis=0, tiled=True),
        lax.all_gather(lowered[2], ("clip", "seq"), axis=0, tiled=True),
        lax.all_gather(lowered[3], ("clip", "seq"), axis=2, tiled=True),
        lax.all_gather(lowered[4], ("clip", "seq"), axis=1, tiled=True),
        lax.all_gather(lowered[5], ("clip", "seq"), axis=0, tiled=True),
        lax.all_gather(lowered[6], ("clip", "seq"), axis=0, tiled=True),
        lax.all_gather(lowered[7], ("clip", "seq"), axis=0, tiled=True),
        lax.all_gather(lowered[8], ("clip", "seq"), axis=0, tiled=True),
        lax.all_gather(lowered[9], ("clip", "seq"), axis=2, tiled=True),
        lax.all_gather(lowered[10], ("clip", "seq"), axis=1, tiled=True),
        lax.all_gather(lowered[11], ("clip", "seq"), axis=0, tiled=True),
        lax.all_gather(lowered[12], ("clip", "seq"), axis=0, tiled=True),
        lax.all_gather(lowered[13], ("clip", "seq"), axis=0, tiled=True),
        lax.all_gather(lowered[14], ("clip", "seq"), axis=0, tiled=True),
        lax.all_gather(lowered[15], ("clip", "seq"), axis=1, tiled=True),
        lax.all_gather(lowered[16], ("clip", "seq"), axis=1, tiled=True),
        lax.all_gather(lowered[17], ("clip", "seq"), axis=0, tiled=True),
    )


def gather_backward(lowered):
    return (
        lax.all_gather(lowered[0], ("clip", "seq"), axis=0, tiled=True),
        lax.all_gather(lowered[1], ("clip", "seq"), axis=0, tiled=True),
        lax.all_gather(lowered[2], ("clip", "seq"), axis=0, tiled=True),
        lax.all_gather(lowered[3], ("clip", "seq"), axis=2, tiled=True),
        lax.all_gather(lowered[4], ("clip", "seq"), axis=1, tiled=True),
        lax.all_gather(lowered[5], ("clip", "seq"), axis=0, tiled=True),
        lax.all_gather(lowered[6], ("clip", "seq"), axis=0, tiled=True),
        lax.all_gather(lowered[7], ("clip", "seq"), axis=0, tiled=True),
        lax.all_gather(lowered[8], ("clip", "seq"), axis=0, tiled=True),
        lax.all_gather(lowered[9], ("clip", "seq"), axis=2, tiled=True),
        lax.all_gather(lowered[10], ("clip", "seq"), axis=1, tiled=True),
        lax.all_gather(lowered[11], ("clip", "seq"), axis=0, tiled=True),
        lax.all_gather(lowered[12], ("clip", "seq"), axis=0, tiled=True),
        lax.all_gather(lowered[13], ("clip", "seq"), axis=0, tiled=True),
        lax.all_gather(lowered[14], ("clip", "seq"), axis=0, tiled=True),
        lax.all_gather(lowered[15], ("clip", "seq"), axis=1, tiled=True),
        lax.all_gather(lowered[16], ("clip", "seq"), axis=1, tiled=True),
        lax.all_gather(lowered[17], ("clip", "seq"), axis=0, tiled=True),
    )


def body(
    inputs,
    space_gain,
    space_shift,
    space_proj,
    space_bias,
    space_out,
    space_out_bias,
    time_gain,
    time_shift,
    time_proj,
    time_bias,
    time_out,
    time_out_bias,
    dense_gain,
    dense_shift,
    dense_in,
    dense_bias,
    dense_out,
    dense_out_bias,
    cotangent,
):
    masters = (
        space_gain,
        space_shift,
        space_proj,
        space_bias,
        space_out,
        space_out_bias,
        time_gain,
        time_shift,
        time_proj,
        time_bias,
        time_out,
        time_out_bias,
        dense_gain,
        dense_shift,
        dense_in,
        dense_bias,
        dense_out,
        dense_out_bias,
    )
    lowered = [master.astype(jnp.bfloat16) for master in masters]
    weights = gather_forward(lowered)
    model_width = inputs.shape[-1]
    space_set = weights[0:6]
    normed_space = layer_norm(
        inputs, space_set[0].astype(jnp.float32), space_set[1].astype(jnp.float32)
    ).astype(jnp.bfloat16)
    merged_space = project_in(normed_space, space_set[2], space_set[3])
    mixed_space, total_space = attend(merged_space, ACROSS_PLACES)
    after_space = inputs + project_out(mixed_space, space_set[4], space_set[5])
    time_set = weights[6:12]
    stream_time = to_places(after_space)
    normed_time = layer_norm(
        stream_time, time_set[0].astype(jnp.float32), time_set[1].astype(jnp.float32)
    ).astype(jnp.bfloat16)
    merged_local = project_in(normed_time, time_set[2], time_set[3])
    mixed_time, total_time = attend(merged_local, ACROSS_FRAMES)
    joined = stream_time + project_out(mixed_time, time_set[4], time_set[5])
    after_time = to_frames(joined)
    dense_set = weights[12:18]
    normed_dense = layer_norm(
        after_time, dense_set[0].astype(jnp.float32), dense_set[1].astype(jnp.float32)
    ).astype(jnp.bfloat16)
    normed_flat = normed_dense.reshape(-1, model_width)
    hidden_width = dense_set[2].shape[1]
    pre_dense = jnp.dot(normed_flat, dense_set[2], preferred_element_type=jnp.float32) + dense_set[
        3
    ].reshape(1, hidden_width).astype(jnp.float32)
    act_dense = jax.nn.gelu(pre_dense, approximate=False).astype(jnp.bfloat16)
    outputs = after_time + project_out(act_dense, dense_set[4], dense_set[5]).reshape(
        after_time.shape
    )
    weights = gather_backward(lowered)
    space_set = weights[0:6]
    time_set = weights[6:12]
    dense_set = weights[12:18]
    grad_rows = cotangent.reshape(-1, model_width)
    grad_dense_out_bias = jnp.sum(grad_rows, axis=0)
    grad_low = grad_rows.astype(jnp.bfloat16)
    grad_dense_out = product("nf,nd->fd", act_dense, grad_low)
    grad_act = product("nd,fd->nf", grad_low, dense_set[4]).astype(jnp.bfloat16)
    outcome, gelu_pull = jax.vjp(lambda values: jax.nn.gelu(values, approximate=False), pre_dense)
    grad_pre = gelu_pull(grad_act.astype(jnp.float32))[0]
    grad_dense_bias = jnp.sum(grad_pre, axis=0).reshape(dense_set[3].shape)
    grad_pre_low = grad_pre.astype(jnp.bfloat16)
    grad_dense_in = product("nd,nf->df", normed_flat, grad_pre_low)
    grad_normed_dense = head_total(product("nf,df->nd", grad_pre_low, dense_set[2])).reshape(
        after_time.shape
    )
    grad_after, grad_dense_gain, grad_dense_shift = norm_back(
        after_time, dense_set[0], dense_set[1], grad_normed_dense
    )
    grad_time_stream = cotangent + grad_after
    grad_time_local = to_places(grad_time_stream)
    grad_time_out_bias, grad_time_out, grad_mixed = out_back(
        grad_time_local, mixed_time, time_set[4]
    )
    grad_merged_time = attend_back(merged_local, total_time, grad_mixed, ACROSS_FRAMES)
    grad_time_proj, grad_time_bias, grad_normed_time = in_back(
        grad_merged_time, normed_time, time_set[2], time_set[3].shape
    )
    grad_stream_part, grad_time_gain, grad_time_shift = norm_back(
        stream_time, time_set[0], time_set[1], grad_normed_time
    )
    grad_joined = grad_time_local + grad_stream_part
    grad_space_stream = to_frames(grad_joined)
    grad_space_out_bias, grad_space_out, grad_mixed_space = out_back(
        grad_space_stream, mixed_space, space_set[4]
    )
    grad_merged_space = attend_back(merged_space, total_space, grad_mixed_space, ACROSS_PLACES)
    grad_space_proj, grad_space_bias, grad_normed_space = in_back(
        grad_merged_space, normed_space, space_set[2], space_set[3].shape
    )
    grad_input_part, grad_space_gain, grad_space_shift = norm_back(
        inputs, space_set[0], space_set[1], grad_normed_space
    )
    input_grad = grad_space_stream + grad_input_part
    shards = (
        lax.psum_scatter(grad_space_gain, ("clip", "seq"), scatter_dimension=0, tiled=True),
        lax.psum_scatter(grad_space_shift, ("clip", "seq"), scatter_dimension=0, tiled=True),
        lax.psum_scatter(grad_space_proj, ("clip", "seq"), scatter_dimension=0, tiled=True),
        lax.psum_scatter(grad_space_bias, ("clip", "seq"), scatter_dimension=2, tiled=True),
        lax.psum_scatter(grad_space_out, ("clip", "seq"), scatter_dimension=1, tiled=True),
        lax.psum_scatter(grad_space_out_bias, ("clip", "seq"), scatter_dimension=0, tiled=True),
        lax.psum_scatter(grad_time_gain, ("clip", "seq"), scatter_dimension=0, tiled=True),
        lax.psum_scatter(grad_time_shift, ("clip", "seq"), scatter_dimension=0, tiled=True),
        lax.psum_scatter(grad_time_proj, ("clip", "seq"), scatter_dimension=0, tiled=True),
        lax.psum_scatter(grad_time_bias, ("clip", "seq"), scatter_dimension=2, tiled=True),
        lax.psum_scatter(grad_time_out, ("clip", "seq"), scatter_dimension=1, tiled=True),
        lax.psum_scatter(grad_time_out_bias, ("clip", "seq"), scatter_dimension=0, tiled=True),
        lax.psum_scatter(grad_dense_gain, ("clip", "seq"), scatter_dimension=0, tiled=True),
        lax.psum_scatter(grad_dense_shift, ("clip", "seq"), scatter_dimension=0, tiled=True),
        lax.psum_scatter(grad_dense_in, ("clip", "seq"), scatter_dimension=0, tiled=True),
        lax.psum_scatter(grad_dense_bias, ("clip", "seq"), scatter_dimension=1, tiled=True),
        lax.psum_scatter(grad_dense_out, ("clip", "seq"), scatter_dimension=1, tiled=True),
        lax.psum_scatter(grad_dense_out_bias, ("clip", "seq"), scatter_dimension=0, tiled=True),
    )
    return (outputs, input_grad) + tuple(shards)


def solution(mesh):
    placed = (
        P("clip", "seq", None, None),
        P(("clip", "seq")),
        P(("clip", "seq")),
        P(("clip", "seq"), None, "head"),
        P(None, "head", ("clip", "seq")),
        P("head", ("clip", "seq")),
        P(("clip", "seq")),
        P(("clip", "seq")),
        P(("clip", "seq")),
        P(("clip", "seq"), None, "head"),
        P(None, "head", ("clip", "seq")),
        P("head", ("clip", "seq")),
        P(("clip", "seq")),
        P(("clip", "seq")),
        P(("clip", "seq")),
        P(("clip", "seq"), "head"),
        P("head", ("clip", "seq")),
        P("head", ("clip", "seq")),
        P(("clip", "seq")),
        P("clip", "seq", None, None),
    )
    return jax.shard_map(
        body,
        mesh=mesh,
        in_specs=placed,
        out_specs=(
            P("clip", "seq", None, None),
            P("clip", "seq", None, None),
            P(("clip", "seq")),
            P(("clip", "seq")),
            P(("clip", "seq"), None, "head"),
            P(None, "head", ("clip", "seq")),
            P("head", ("clip", "seq")),
            P(("clip", "seq")),
            P(("clip", "seq")),
            P(("clip", "seq")),
            P(("clip", "seq"), None, "head"),
            P(None, "head", ("clip", "seq")),
            P("head", ("clip", "seq")),
            P(("clip", "seq")),
            P(("clip", "seq")),
            P(("clip", "seq")),
            P(("clip", "seq"), "head"),
            P("head", ("clip", "seq")),
            P("head", ("clip", "seq")),
            P(("clip", "seq")),
        ),
        check_vma=False,
    )
```

profile of v0, /device:TPU:0, one launch (start us, length us, event | category | flops | bytes accessed | tf_op | source)
XLA Modules:
  0.0 1186.6 jit_solution(11910681866152128916)
XLA Ops:
  18.9 63.1 %all-reduce.22 = (bf16[768]{0:T(1024)(128)(2,1)S(1)}, bf16[768]{0:T(1024)(128)(2,1)S(1)}, bf16[768]{0:T(1024)(128)(2,1)S(1)}, bf16[768]{0:T(1024)(128)(2,1)S(1)}...) all-reduce(bf16[768]{0:T(1024)(128)(2,1)S(1)} %dynamic-update-slice, ...), channel_id=1, replica_groups=mesh['clip'=4,'seq'=4,'head'=2] {'clip','seq'}, use_global_device_ids=true, to_apply=%add.1 | all-reduce | flops 6912 | bytes 27648
  90.2 17.3 %all_gather.72 = bf16[2,3,128]{1,0,2:T(2,128)(2,1)S(1)} all-gather(bf16[2,3,8]{1,0,2:T(2,128)(2,1)S(1)} %copy.629), channel_id=1, replica_groups=mesh['clip'=4,'seq'=4,'head'=2] {'clip','seq'}, dimensions={2}, use_global_device_ids=true | all-gather | bytes 1632 | tf_op jit(solution)/shard_map/all_gather | solution.py:159
  107.9 19.2 %all_gather.66 = bf16[2,3,128]{1,0,2:T(2,128)(2,1)S(1)} all-gather(bf16[2,3,8]{1,0,2:T(2,128)(2,1)S(1)} %copy.611), channel_id=1, replica_groups=mesh['clip'=4,'seq'=4,'head'=2] {'clip','seq'}, dimensions={2}, use_global_device_ids=true | all-gather | bytes 1632 | tf_op jit(solution)/shard_map/all_gather | solution.py:153
  127.6 20.7 %all_gather.67 = bf16[384,768]{0,1:T(8,128)(2,1)} all-gather(bf16[384,48]{0,1:T(8,128)(2,1)S(1)} %convert_element_type.482), channel_id=1, replica_groups=mesh['clip'=4,'seq'=4,'head'=2] {'clip','seq'}, dimensions={1}, use_global_device_ids=true | all-gather | bytes 626688 | tf_op jit(solution)/shard_map/all_gather | solution.py:154
  148.2 3.8 copy.610
  152.1 4.8 fusion.13
  156.9 6.4 reshape.1185
  163.3 5.0 fusion.76
  183.3 3.1 convolution_convert_fusion.5
  187.2 41.5 %all-reduce.30.cloned.1.call-done = bf16[784,768]{1,0:T(8,128)(2,1)} async-done(((bf16[784,768]{1,0:T(8,128)(2,1)}), bf16[784,768]{1,0:T(8,128)(2,1)}) %all-reduce.30.cloned.1.call-update) | async-done | bytes 1204240 | tf_op jit(solution)/shard_map/psum | solution.py:83
  238.0 3.5 all-to-all-start
  241.7 34.9 %all_gather.73 = bf16[384,768]{0,1:T(8,128)(2,1)} all-gather(bf16[384,48]{0,1:T(8,128)(2,1)S(1)} %convert_element_type.507), channel_id=1, replica_groups=mesh['clip'=4,'seq'=4,'head'=2] {'clip','seq'}, dimensions={1}, use_global_device_ids=true | all-gather | bytes 626688 | tf_op jit(solution)/shard_map/all_gather | solution.py:160
  276.6 3.9 copy.628
  285.1 4.8 fusion.14
  289.9 6.4 reshape_reshape.10
  296.4 3.2 fusion.75
  305.1 3.1 convolution_convert_fusion.3
  313.4 36.0 %all-reduce.32.cloned.1.call-done = bf16[784,768]{1,0:T(8,128)(2,1)} async-done(((bf16[784,768]{1,0:T(8,128)(2,1)}), bf16[784,768]{1,0:T(8,128)(2,1)}) %all-reduce.32.cloned.1.call-update) | async-done | bytes 1204240 | tf_op jit(solution)/shard_map/psum | solution.py:83
  359.2 4.3 all-to-all-start.1
  364.4 32.6 %all_gather.78 = bf16[12,128]{0,1:T(8,128)(2,1)S(1)} all-gather(bf16[12,8]{0,1:T(8,128)(2,1)S(1)} %convert_element_type.526), channel_id=1, replica_groups=mesh['clip'=4,'seq'=4,'head'=2] {'clip','seq'}, dimensions={1}, use_global_device_ids=true | all-gather | bytes 3264 | tf_op jit(solution)/shard_map/all_gather | solution.py:165
  399.6 3.9 reshape.1115
  405.5 12.1 %multiply_reduce_fusion.7 = f32[4,4,49]{2,0,1:T(4,128)S(1)} fusion(f32[4,4,49]{2,0,1:T(4,128)S(1)} %copy.643, f32[1,4,4,49,768]{4,0,3,2,1:T(1,128)S(1)} %reshape.1115), kind=kLoop, calls=%fused_computation.85 | loop fusion | flops 1805552 | bytes 2414720 | tf_op jit(solution)/shard_map/reduce_sum | solution.py:21
  422.4 16.4 %multiply_convert_fusion.1 = (bf16[784,1536]{1,0:T(8,128)(2,1)}, f32[784,1536]{1,0:T(8,128)}, f32[784,1536]{1,0:T(8,128)}) fusion(f32[1536]{0:T(1024)S(1)} %bitcast_convert_fusion, bf16[768,1536]{1,0:T(8,128)(2,1)} %all-gather.9.cloned.1.call-done, f32[784,768]{1,0:T(8,128)} %reshape.1107, f32[768]{0:T(1024)S(1)} %convert_element_type.523, ...), kind=kOutput, calls=%fused_computation.17 | convolution fusion | flops 1932177408 | bytes 16828544 | tf_op jit(solution)/shard_map/dot_general | solution.py:261
  439.4 9.0 fusion.85
  449.8 3.1 convolution_convert_fusion.6
  455.2 40.0 %all-reduce.34.cloned.1.call-done = bf16[784,768]{1,0:T(8,128)(2,1)} async-done(((bf16[784,768]{1,0:T(8,128)(2,1)}), bf16[784,768]{1,0:T(8,128)(2,1)}) %all-reduce.34.cloned.1.call-update) | async-done | bytes 1204240 | tf_op jit(solution)/shard_map/psum | solution.py:83
  498.0 7.3 fusion.36
  505.8 3.2 multiply_reduce_fusion.2
  512.1 7.1 fusion.52
  519.2 3.7 all-to-all-start.2
  523.0 16.0 %all-to-all-done.2 = bf16[1,4,196,768]{3,1,0,2:T(4,128)(2,1)S(1)} async-done(((bf16[1,4,196,768]{3,1,0,2:T(4,128)(2,1)}), bf16[1,4,196,768]{3,1,0,2:T(4,128)(2,1)S(1)}, u32[]{:S(2)}, u32[]{:S(2)}) %all-to-all-start.2) | async-done | bytes 1204256 | tf_op jit(solution)/shard_map/all_to_all | solution.py:137
  557.0 3.4 copy.662
  560.5 7.0 convert_element_type.549
  567.4 4.9 convolution_convert_fusion.2
  574.5 3.1 reshape.1110
  579.9 3.6 reshape.1109
  583.6 31.7 %all-reduce.36.cloned.1.call-done = bf16[784,768]{1,0:T(8,128)(2,1)} async-done(((bf16[784,768]{1,0:T(8,128)(2,1)}), bf16[784,768]{1,0:T(8,128)(2,1)}) %all-reduce.36.cloned.1.call-update) | async-done | bytes 1204240 | tf_op jit(solution)/shard_map/psum | solution.py:83
  618.2 3.5 fusion.31
  628.1 3.3 fusion.28
  632.9 3.5 all-to-all-start.3
  636.5 5.5 convolution_convert_fusion.7
  642.1 12.3 %all-to-all-done.3 = bf16[1,16,49,768]{3,2,0,1:T(8,128)(2,1)S(1)} async-done(((bf16[1,16,49,768]{3,2,0,1:T(8,128)(2,1)}), bf16[1,16,49,768]{3,2,0,1:T(8,128)(2,1)S(1)}, u32[]{:S(2)}, u32[]{:S(2)}) %all-to-all-start.3) | async-done | bytes 1204256 | tf_op jit(solution)/shard_map/all_to_all | solution.py:143
  662.8 4.2 multiply_reduce_fusion
  672.0 3.4 copy.683
  675.4 5.4 convert_element_type.561
  680.8 5.0 convolution_convert_fusion.1
  686.8 3.3 fusion.89
  690.2 3.6 fusion.87
  693.9 7.5 fusion.48
  702.6 6.0 fusion.90
  711.3 4.1 copy.691
  715.4 5.7 fusion.88
  723.5 6.0 fusion.86
  733.5 21.4 %all-reduce.38.cloned.1.call-done = (bf16[784,768]{1,0:T(8,128)(2,1)}, bf16[784,768]{1,0:T(8,128)(2,1)}) async-done(((bf16[784,768]{1,0:T(8,128)(2,1)}, bf16[784,768]{1,0:T(8,128)(2,1)}), (bf16[784,768]{1,0:T(8,128)(2,1)}, bf16[784,768]{1,0:T(8,128)(2,1)})) %all-reduce.38.cloned.1.call-update) | async-done | bytes 2408464 | tf_op jit(solution)/shard_map/psum | solution.py:83
  757.6 3.2 multiply_reduce_fusion.5
  762.6 5.8 multiply_reduce_fusion.4
  768.4 61.4 %all-reduce.21 = (f32[768]{0:T(1024)S(1)}, f32[768]{0:T(1024)S(1)}, f32[2,3,128]{2,1,0:T(4,128)S(1)}, f32[768]{0:T(1024)S(1)}, f32[768]{0:T(1024)S(1)}, /*index=...) all-reduce(f32[768]{0:T(1024)S(1)} %get-tuple-element.200, ...), channel_id=2, replica_groups=mesh['clip'=4,'seq'=4,'head'=2] {'clip','seq'}, use_global_device_ids=true, to_apply=%region_25.0.clone | all-reduce | flops 9984 | bytes 79872
  842.8 5.2 copy_add_fusion.1
  848.0 3.4 add_add_fusion.5
  851.4 27.4 %reduce-scatter.12.cloned.1.call-done = f32[384,48]{0,1:T(8,128)} async-done(((f32[384,768]{0,1:T(8,128)}), f32[384,48]{0,1:T(8,128)}) %reduce-scatter.12.cloned.1.call-update) | async-done | bytes 73744 | tf_op jit(solution)/shard_map/reduce_scatter | solution.py:318
  878.8 78.9 %reduce-scatter.18.cloned.1.call-done = f32[48,1536]{1,0:T(8,128)} async-done(((f32[768,1536]{1,0:T(8,128)}), f32[48,1536]{1,0:T(8,128)}) %reduce-scatter.18.cloned.1.call-update) | async-done | bytes 294928 | tf_op jit(solution)/shard_map/reduce_scatter | solution.py:328
  957.7 79.2 %reduce-scatter.20.cloned.1.call-done = f32[1536,48]{0,1:T(8,128)} async-done(((f32[1536,768]{0,1:T(8,128)}), f32[1536,48]{0,1:T(8,128)}) %reduce-scatter.20.cloned.1.call-update) | async-done | bytes 294928 | tf_op jit(solution)/shard_map/reduce_scatter | solution.py:330
  1036.9 71.7 %reduce-scatter.14.cloned.1.call-done = f32[48,3,384]{2,0,1:T(8,128)} async-done(((f32[768,3,384]{2,0,1:T(8,128)}), f32[48,3,384]{2,0,1:T(8,128)}) %reduce-scatter.14.cloned.1.call-update) | async-done | bytes 221200 | tf_op jit(solution)/shard_map/reduce_scatter | solution.py:322
  1108.6 71.3 %reduce-scatter.10.cloned.1.call-done = f32[48,3,384]{2,0,1:T(8,128)} async-done(((f32[768,3,384]{2,0,1:T(8,128)}), f32[48,3,384]{2,0,1:T(8,128)}) %reduce-scatter.10.cloned.1.call-update) | async-done | bytes 221200 | tf_op jit(solution)/shard_map/reduce_scatter | solution.py:316
  (390 shorter events, 164.7 us)
Async XLA Ops:
  7.2 76.9 %copy-start.1 = (f32[1,4,196,768]{3,1,2,0:T(4,128)S(1)}, f32[1,4,196,768]{3,1,2,0:T(4,128)}, u32[]{:S(2)}) copy-start(f32[1,4,196,768]{3,1,2,0:T(4,128)} %param.20) | copy-start | bytes 7225348
  7.2 141.0 %all-gather.5.cloned.1.call-start = ((), (), s32[]{:S(2)}) async-start(), calls=%async_computation.10 | async-start | bytes 1880064 | tf_op jit(solution)/shard_map/all_gather | solution.py:152
  9.0 219.7 %all-reduce.30.cloned.1.call-start = ((), (), s32[]{:S(2)}) async-start(), calls=%async_computation.11 | async-start | bytes 2408448 | tf_op jit(solution)/shard_map/psum | solution.py:83
  82.0 3.2 copy-start.54
  84.1 2.6 copy-start.31
  86.7 3.4 copy-start.65
  86.7 21.0 %copy-start.66 = (f32[2,3,8]{2,0,1:T(2,128)S(1)}, f32[2,3,8]{2,0,1:T(2,128)}, u32[]{:S(2)}) copy-start(f32[2,3,8]{2,0,1:T(2,128)} %param.24) | copy-start | bytes 580
  86.7 40.8 %copy-start.56 = (f32[384,48]{0,1:T(8,128)S(1)}, f32[384,48]{0,1:T(8,128)}, u32[]{:S(2)}) copy-start(f32[384,48]{0,1:T(8,128)} %param.25) | copy-start | bytes 221188
  170.2 7.6 copy-start.27
  181.8 4.7 copy-start.51
  186.4 90.1 %all-gather.7.cloned.1.call-start = ((), (), s32[]{:S(2)}) async-start(), calls=%async_computation.12 | async-start | bytes 1880064 | tf_op jit(solution)/shard_map/all_gather | solution.py:158
  236.5 5.1 copy-start.57
  238.0 42.4 %all-to-all-start = ((bf16[1,4,196,768]{3,1,0,2:T(4,128)(2,1)}), bf16[1,4,196,768]{3,1,0,2:T(4,128)(2,1)S(1)}, u32[]{:S(2)}, u32[]{:S(2)}) async-start(bf16[1,4,196,768]{3,1,0,2:T(4,128)(2,1)} %copy.621), calls=%async_computation | async-start | bytes 2408448 | tf_op jit(solution)/shard_map/all_to_all | solution.py:137
  241.6 107.8 %all-reduce.32.cloned.1.call-start = ((), (), s32[]{:S(2)}) async-start(), calls=%async_computation.13 | async-start | bytes 2408448 | tf_op jit(solution)/shard_map/psum | solution.py:83
  280.4 28.6 %copy-start.5 = (bf16[1,4,196,768]{3,1,0,2:T(4,128)(2,1)}, bf16[1,4,196,768]{3,1,0,2:T(4,128)(2,1)S(1)}, u32[]{:S(2)}) copy-start(bf16[1,4,196,768]{3,1,0,2:T(4,128)(2,1)S(1)} %all-to-all-done) | copy-start | bytes 3612676
  283.6 6.3 copy-start.16
  305.1 4.3 copy-start.35
  305.1 3.2 copy-start.49
  308.3 114.1 %all-gather.9.cloned.1.call-start = ((), (), s32[]{:S(2)}) async-start(), calls=%async_computation.14 | async-start | bytes 2506752 | tf_op jit(solution)/shard_map/all_gather | solution.py:164
  313.3 41.8 %copy-start.9 = (f32[1,4,4,49,768]{4,0,3,2,1:T(1,128)}, f32[1,4,4,49,768]{4,0,3,2,1:T(1,128)S(1)}, u32[]{:S(2)}) copy-start(f32[1,4,4,49,768]{4,0,3,2,1:T(1,128)S(1)} %copy.622) | copy-start | bytes 7225348
  357.7 5.9 copy-start.50
  357.7 6.6 copy-start.62
  357.7 39.4 %copy-start.25 = (f32[1,4,196,768]{3,1,2,0:T(4,128)S(1)}, f32[1,4,196,768]{3,1,2,0:T(4,128)}, u32[]{:S(2)}) copy-start(f32[1,4,196,768]{3,1,2,0:T(4,128)} %param.39) | copy-start | bytes 7225348
  359.2 40.4 %all-to-all-start.1 = ((bf16[1,16,49,768]{3,2,0,1:T(8,128)(2,1)}), bf16[1,16,49,768]{3,2,0,1:T(8,128)(2,1)}, u32[]{:S(2)}, u32[]{:S(2)}) async-start(bf16[1,16,49,768]{3,2,0,1:T(8,128)(2,1)} %copy.639), calls=%async_computation.1 | async-start | bytes 2752512 | tf_op jit(solution)/shard_map/all_to_all | solution.py:143
  363.5 75.9 %all-gather.11.cloned.1.call-start = ((), (), s32[]{:S(2)}) async-start(), calls=%async_computation.15 | async-start | bytes 2506752 | tf_op jit(solution)/shard_map/all_gather | solution.py:166
  364.3 131.0 %all-reduce.34.cloned.1.call-start = ((), (), s32[]{:S(2)}) async-start(), calls=%async_computation.16 | async-start | bytes 2408448 | tf_op jit(solution)/shard_map/psum | solution.py:83
  364.4 58.0 %copy-start.63 = (f32[768]{0:T(1024)}, f32[768]{0:T(1024)S(1)}, u32[]{:S(2)}) copy-start(f32[768]{0:T(1024)S(1)} %convert_element_type.523) | copy-start | bytes 9220
  439.4 10.4 copy-start.68
  509.1 3.0 copy-start.8
  519.2 3.7 copy-start.40
  519.2 3.7 copy-start.46
  519.2 19.7 %all-to-all-start.2 = ((bf16[1,4,196,768]{3,1,0,2:T(4,128)(2,1)}), bf16[1,4,196,768]{3,1,0,2:T(4,128)(2,1)S(1)}, u32[]{:S(2)}, u32[]{:S(2)}) async-start(bf16[1,4,196,768]{3,1,0,2:T(4,128)(2,1)} %fusion.52), calls=%async_computation.2 | async-start | bytes 2408448 | tf_op jit(solution)/shard_map/all_to_all | solution.py:137
  522.8 92.4 %all-reduce.36.cloned.1.call-start = ((), (), s32[]{:S(2)}) async-start(), calls=%async_computation.17 | async-start | bytes 2408448 | tf_op jit(solution)/shard_map/psum | solution.py:83
  538.9 2.7 copy-start.38
  541.6 6.1 copy-start.4
  567.4 4.9 copy-start.12
  574.5 3.3 copy-start.14
  583.6 34.6 %copy-start.6 = (bf16[1,4,196,768]{3,1,0,2:T(4,128)(2,1)S(1)}, bf16[1,4,196,768]{3,1,0,2:T(4,128)(2,1)}, u32[]{:S(2)}) copy-start(bf16[1,4,196,768]{3,1,0,2:T(4,128)(2,1)} %copy-done.5) | copy-start | bytes 3612676
  618.2 3.9 copy-start.19
  625.1 3.1 copy-start.10
  631.4 5.1 copy-start.48
  631.5 5.1 copy-start.53
  632.9 21.5 %all-to-all-start.3 = ((bf16[1,16,49,768]{3,2,0,1:T(8,128)(2,1)}), bf16[1,16,49,768]{3,2,0,1:T(8,128)(2,1)S(1)}, u32[]{:S(2)}, u32[]{:S(2)}) async-start(bf16[1,16,49,768]{3,2,0,1:T(8,128)(2,1)} %copy.673), calls=%async_computation.3 | async-start | bytes 2752512 | tf_op jit(solution)/shard_map/all_to_all | solution.py:143
  636.5 118.5 %all-reduce.38.cloned.1.call-start = ((), (), s32[]{:S(2)}) async-start(), calls=%async_computation.24 | async-start | bytes 4816896 | tf_op jit(solution)/shard_map/psum | solution.py:83
  660.8 6.2 slice-start
  662.8 4.2 slice-start.1
  685.8 4.4 copy-start.34
  685.8 165.6 %reduce-scatter.16.cloned.1.call-start = ((), (), s32[]{:S(2)}) async-start(), calls=%async_computation.21 | async-start | bytes 1253376 | tf_op jit(solution)/shard_map/reduce_scatter | solution.py:324
  690.1 3.7 copy-start.64
  690.1 188.6 %reduce-scatter.12.cloned.1.call-start = ((), (), s32[]{:S(2)}) async-start(), calls=%async_computation.19 | async-start | bytes 1253376 | tf_op jit(solution)/shard_map/reduce_scatter | solution.py:318
  693.8 263.9 %reduce-scatter.18.cloned.1.call-start = ((), (), s32[]{:S(2)}) async-start(), calls=%async_computation.22 | async-start | bytes 5013504 | tf_op jit(solution)/shard_map/reduce_scatter | solution.py:328
  701.4 335.5 %reduce-scatter.20.cloned.1.call-start = ((), (), s32[]{:S(2)}) async-start(), calls=%async_computation.23 | async-start | bytes 5013504 | tf_op jit(solution)/shard_map/reduce_scatter | solution.py:330
  708.7 399.9 %reduce-scatter.14.cloned.1.call-start = ((), (), s32[]{:S(2)}) async-start(), calls=%async_computation.20 | async-start | bytes 3760128 | tf_op jit(solution)/shard_map/reduce_scatter | solution.py:322
  711.3 4.1 copy-start.43
  721.0 458.9 %reduce-scatter.10.cloned.1.call-start = ((), (), s32[]{:S(2)}) async-start(), calls=%async_computation.18 | async-start | bytes 3760128 | tf_op jit(solution)/shard_map/reduce_scatter | solution.py:316
  733.3 24.2 %copy-start.2 = (f32[1,4,196,768]{3,1,2,0:T(4,128)S(1)}, f32[1,4,196,768]{3,1,2,0:T(4,128)}, u32[]{:S(2)}) copy-start(f32[1,4,196,768]{3,1,2,0:T(4,128)} %param.20) | copy-start | bytes 7225348
  733.3 24.2 %copy-start.32 = (f32[4,196]{0,1:T(8,128)S(1)}, f32[4,196]{0,1:T(8,128)}, u32[]{:S(2)}) copy-start(f32[4,196]{0,1:T(8,128)} %copy-done.31) | copy-start | bytes 9412
  733.3 24.2 %copy-start.55 = (f32[768]{0:T(1024)S(1)}, f32[768]{0:T(1024)}, u32[]{:S(2)}) copy-start(f32[768]{0:T(1024)} %copy-done.54) | copy-start | bytes 9220
  757.6 3.3 copy-start.59
  757.6 5.0 copy-start.42
  762.6 5.8 copy-start.60
  762.6 5.8 copy-start.61
  842.8 5.2 copy-start.7
  842.8 5.2 copy-start.26
  (27 other events, 40.6 us)
Sparse Core Ops, SparseCore 0:
  10.9 43.1 all-gather.4
  186.6 42.0 all-reduce.29
  231.6 42.8 all-gather.6
  308.4 40.9 all-reduce.31
  352.1 44.3 all-gather.8
  399.1 40.2 all-gather.10
  453.0 42.2 all-reduce.33
  572.5 42.7 all-reduce.35
  685.9 68.9 all-reduce.37
  759.0 58.3 reduce-scatter.15
  821.5 57.1 reduce-scatter.11
  883.1 74.5 reduce-scatter.17
  962.1 74.7 reduce-scatter.19
  1041.2 67.3 reduce-scatter.13
  1112.9 66.9 reduce-scatter.9
where the time goes:
time: 1190 us
  waiting for transfers between devices  528 us (44%)
  blocking collectives  249 us (21%)
  local copies, waits for them, and re-layouts  163 us (14%)
  matrix products  114 us (10%)
  other arithmetic  99.1 us (8%)
  between operations  17.5 us (1%)
  starting transfers between devices  16.3 us (1%)
    psum x5, waiting for transfers between devices, head_total(): lax.psum(partial_rows.astype(jnp.bfloat16), 'head').astype(jnp.float32)  171 us
    unnamed x2, blocking collectives  125 us
    reduce_scatter x1, waiting for transfers between devices, body(): lax.psum_scatter(grad_dense_out, ('clip', 'seq'), scatter_dimension=1, ti...  79.2 us
    reduce_scatter x1, waiting for transfers between devices, body(): lax.psum_scatter(grad_dense_in, ('clip', 'seq'), scatter_dimension=0, til...  78.9 us
    dot_general x24, matrix products, product(): return jnp.einsum(form, left, right, preferred_element_type=jnp.float32)  75.8 us
    reduce_scatter x1, waiting for transfers between devices, body(): lax.psum_scatter(grad_time_proj, ('clip', 'seq'), scatter_dimension=0, ti...  71.7 us
    reduce_scatter x1, waiting for transfers between devices, body(): lax.psum_scatter(grad_space_proj, ('clip', 'seq'), scatter_dimension=0, t...  71.3 us
    all_gather x1, blocking collectives, gather_forward(): lax.all_gather(lowered[10], ('clip', 'seq'), axis=1, tiled=True)  34.9 us
  transfers between devices with their start and end apart: 19, of which 13 were waited for; matrix products, arithmetic and copies ran while one was open for 15% of the time, Pallas kernels for 0%

commit v1 on v0

v1 whole, which is shorter than its diff:
```python
import jax
import jax.numpy as jnp
from jax import lax
from jax.sharding import PartitionSpec as P

HEAD_DIM = 64
NORM_EPS = 1e-06
BF = jnp.bfloat16
F32 = jnp.float32
SHARDS = ("head", "clip", "seq")
PLACE_AXES = ("seq", "head")


def product(form, left, right):
    return jnp.einsum(form, left, right, preferred_element_type=F32)


def norm_stats(values):
    mean = jnp.mean(values, axis=-1, keepdims=True)
    centred = values - mean
    spread = jnp.mean(centred * centred, axis=-1, keepdims=True)
    rate = lax.rsqrt(spread + NORM_EPS)
    return centred * rate, rate


def norm_back(unit, rate, gain, grad_normed):
    grad_gain = jnp.sum(grad_normed * unit, axis=0)
    grad_shift = jnp.sum(grad_normed, axis=0)
    scaled = grad_normed * gain
    inner = jnp.mean(scaled * unit, axis=-1, keepdims=True)
    outer = jnp.mean(scaled, axis=-1, keepdims=True)
    return rate * (scaled - outer - unit * inner), grad_gain, grad_shift


def project_in(normed, weights, bias):
    groups, _, triple = weights.shape
    width = triple // 3
    full = jnp.stack([bias[:, 0], jnp.zeros_like(bias[:, 0]), bias[:, 1]], axis=1)
    rows = product("nd,hdk->hnk", normed, weights) + full.reshape(groups, 1, triple)
    return rows.astype(BF).reshape(groups, normed.shape[0], 3, width)


def split_heads(merged, lead):
    groups = merged.shape[0]
    shaped = merged.reshape((groups,) + lead + (3, merged.shape[-1] // HEAD_DIM, HEAD_DIM))
    return shaped[..., 0, :, :], shaped[..., 1, :, :], shaped[..., 2, :, :]


def attend(merged, lead):
    queries, keys, values = split_heads(merged, lead)
    scores = product("gbqje,gbkje->gbjqk", queries, keys) * HEAD_DIM ** (-0.5)
    weights = jnp.exp(scores - jnp.max(scores, axis=-1, keepdims=True))
    probs = weights / jnp.sum(weights, axis=-1, keepdims=True)
    mixed = product("gbjqk,gbkje->gbqje", probs.astype(BF), values).astype(BF)
    return mixed.reshape(merged.shape[0], merged.shape[1], merged.shape[3]), probs


def attend_back(merged, probs, grad_mixed, lead):
    queries, keys, values = split_heads(merged, lead)
    grad_heads = grad_mixed.reshape(queries.shape)
    grad_values = product("gbjqk,gbqje->gbkje", probs.astype(BF), grad_heads)
    grad_probs = product("gbqje,gbkje->gbjqk", grad_heads, values)
    grad_scores = probs * (grad_probs - jnp.sum(probs * grad_probs, axis=-1, keepdims=True))
    grad_scores = grad_scores.astype(BF)
    scale = HEAD_DIM ** (-0.5)
    grad_queries = product("gbjqk,gbkje->gbqje", grad_scores, keys) * scale
    grad_keys = product("gbjqk,gbqje->gbkje", grad_scores, queries) * scale
    stacked = jnp.stack([grad_queries, grad_keys, grad_values], axis=3).astype(BF)
    return stacked.reshape(merged.shape)


def to_places(rows, count):
    frames, places, width = rows.shape
    share = -(-places // count)
    padded = jnp.pad(rows, ((0, 0), (0, share * count - places), (0, 0)))
    cut = padded.reshape(frames, count, share, width).transpose(1, 0, 2, 3)
    moved = lax.all_to_all(cut, PLACE_AXES, split_axis=0, concat_axis=0, tiled=True)
    return moved.reshape(count * frames, share, width)


def to_frames(rows, count, places):
    total, share, width = rows.shape
    frames = total // count
    cut = rows.reshape(count, frames, share, width)
    moved = lax.all_to_all(cut, PLACE_AXES, split_axis=0, concat_axis=0, tiled=True)
    back = moved.transpose(1, 0, 2, 3).reshape(frames, count * share, width)
    return back[:, :places]


def gather(block):
    return lax.all_gather(block, SHARDS, axis=0, tiled=False)


def body(
    inputs,
    space_gain,
    space_shift,
    space_proj,
    space_bias,
    space_out,
    space_out_bias,
    time_gain,
    time_shift,
    time_proj,
    time_bias,
    time_out,
    time_out_bias,
    dense_gain,
    dense_shift,
    dense_in,
    dense_bias,
    dense_out,
    dense_out_bias,
    cotangent,
):
    n_head = lax.axis_size("head")
    n_own = lax.axis_size("clip") * lax.axis_size("seq")
    count = lax.axis_size("seq") * n_head
    here = lax.axis_index("head")
    _, held, places, width = inputs.shape
    frames = held // n_head
    strip = space_gain.shape[0]

    def block_of(proj, out):
        flat = proj.reshape(strip, -1).astype(BF)
        return jnp.concatenate([flat, out.astype(BF).T], axis=1)

    def whole(block):
        return gather(block).reshape(n_head, width, block.shape[1])

    space_all = whole(block_of(space_proj, space_out))
    time_all = whole(block_of(time_proj, time_out))
    dense_all = whole(block_of(dense_in, dense_out))
    part = space_out.shape[0]
    hidden = dense_out.shape[0]

    vectors = (
        space_gain, space_shift, space_out_bias, time_gain, time_shift, time_out_bias,
        dense_gain, dense_shift, dense_out_bias,
    )
    odd = (space_bias, time_bias, dense_bias)
    small = jnp.concatenate([v.reshape(-1) for v in vectors + odd]).astype(BF)
    small_all = gather(small).reshape(n_head, n_own, -1).astype(F32)
    whole_vectors = []
    for i in range(len(vectors)):
        whole_vectors.append(small_all[0, :, i * strip:(i + 1) * strip].reshape(width))
    at = len(vectors) * strip
    sizes = [v.size for v in odd]
    bias_s = small_all[:, :, at:at + sizes[0]]
    bias_t = small_all[:, :, at + sizes[0]:at + sizes[0] + sizes[1]]
    bias_d = small_all[:, :, at + sizes[0] + sizes[1]:]

    def rows_bias(flat, shape):
        lines, lanes = shape[:-1], shape[-1]
        count_lines = 1
        for n in lines:
            count_lines *= n
        spread = flat.reshape(n_head, n_own, count_lines, lanes).transpose(0, 2, 1, 3)
        return spread.reshape(n_head, lines[0], -1)

    bias_s = rows_bias(bias_s, space_bias.shape)
    bias_t = rows_bias(bias_t, time_bias.shape)
    bias_d = rows_bias(bias_d, dense_bias.shape).reshape(n_head, 1, hidden)
    (g_s, b_s, ob_s, g_t, b_t, ob_t, g_d, b_d, ob_d) = whole_vectors

    own = lax.dynamic_slice_in_dim(inputs[0], here * frames, frames, axis=0)
    own = own.reshape(frames * places, width)
    cot = lax.dynamic_slice_in_dim(cotangent[0], here * frames, frames, axis=0)
    cot = cot.reshape(frames * places, width)

    proj_s, out_s = space_all[..., :3 * part], space_all[..., 3 * part:]
    proj_t, out_t = time_all[..., :3 * part], time_all[..., 3 * part:]
    in_d, out_d = dense_all[..., :hidden], dense_all[..., hidden:]

    unit_s, rate_s = norm_stats(own)
    normed_s = (unit_s * g_s + b_s).astype(BF)
    merged_s = project_in(normed_s, proj_s, bias_s)
    mixed_s, probs_s = attend(merged_s, (frames, places))
    after_space = own + product("hnw,hdw->nd", mixed_s, out_s) + ob_s

    unit_t, rate_t = norm_stats(after_space)
    normed_t = (unit_t * g_t + b_t).astype(BF)
    rows_t = to_places(normed_t.reshape(frames, places, width), count)
    total_frames, share = rows_t.shape[:2]
    rows_t = rows_t.transpose(1, 0, 2).reshape(-1, width)
    lead_t = (share, total_frames)
    merged_t = project_in(rows_t, proj_t, bias_t)
    mixed_t, probs_t = attend(merged_t, lead_t)
    branch_t = product("hnw,hdw->nd", mixed_t, out_t).astype(BF)
    branch_t = to_frames(branch_t.reshape(share, total_frames, width).transpose(1, 0, 2), count, places)
    after_time = after_space + branch_t.reshape(-1, width).astype(F32) + ob_t

    unit_d, rate_d = norm_stats(after_time)
    normed_d = (unit_d * g_d + b_d).astype(BF)
    pre = product("nd,hdk->hnk", normed_d, in_d) + bias_d
    act = jax.nn.gelu(pre, approximate=False).astype(BF)
    result = after_time + product("hnk,hdk->nd", act, out_d) + ob_d

    grad_ob_d = jnp.sum(cot, axis=0)
    low_d = cot.astype(BF)
    grad_out_d = product("nd,hnk->hdk", low_d, act)
    grad_act = product("nd,hdk->hnk", low_d, out_d).astype(BF).astype(F32)
    _, pull = jax.vjp(lambda v: jax.nn.gelu(v, approximate=False), pre)
    grad_pre = pull(grad_act)[0]
    grad_bias_d = jnp.sum(grad_pre, axis=1)
    low_pre = grad_pre.astype(BF)
    grad_in_d = product("nd,hnk->hdk", normed_d, low_pre)
    grad_normed = product("hnk,hdk->nd", low_pre, in_d)
    grad_v, grad_g_d, grad_b_d = norm_back(unit_d, rate_d, g_d, grad_normed)
    stream_t = cot + grad_v

    grad_ob_t = jnp.sum(stream_t, axis=0)
    low_t = to_places(stream_t.astype(BF).reshape(frames, places, width), count)
    low_t = low_t.transpose(1, 0, 2).reshape(-1, width)
    grad_out_t = product("nd,hnw->hdw", low_t, mixed_t)
    grad_mixed = product("nd,hdw->hnw", low_t, out_t).astype(BF)
    grad_merged_t = attend_back(merged_t, probs_t, grad_mixed, lead_t)
    sums_t = jnp.sum(grad_merged_t.astype(F32), axis=1)
    flat_t = grad_merged_t.reshape(n_head, -1, 3 * part)
    grad_proj_t = product("nd,hnk->hdk", rows_t, flat_t)
    grad_rows = product("hnk,hdk->nd", flat_t, proj_t).astype(BF)
    grad_rows = to_frames(grad_rows.reshape(share, total_frames, width).transpose(1, 0, 2), count, places)
    grad_v, grad_g_t, grad_b_t = norm_back(unit_t, rate_t, g_t, grad_rows.reshape(-1, width).astype(F32))
    stream_s = stream_t + grad_v

    grad_ob_s = jnp.sum(stream_s, axis=0)
    low_s = stream_s.astype(BF)
    grad_out_s = product("nd,hnw->hdw", low_s, mixed_s)
    grad_mixed = product("nd,hdw->hnw", low_s, out_s).astype(BF)
    grad_merged_s = attend_back(merged_s, probs_s, grad_mixed, (frames, places))
    sums_s = jnp.sum(grad_merged_s.astype(F32), axis=1)
    flat_s = grad_merged_s.reshape(n_head, -1, 3 * part)
    grad_proj_s = product("nd,hnk->hdk", normed_s, flat_s)
    grad_rows = product("hnk,hdk->nd", flat_s, proj_s)
    grad_v, grad_g_s, grad_b_s = norm_back(unit_s, rate_s, g_s, grad_rows)
    input_own = stream_s + grad_v

    def owners(proj_grad, out_grad):
        both = jnp.concatenate([proj_grad.astype(BF), out_grad.astype(BF)], axis=2)
        mine = lax.psum_scatter(both.reshape(n_head * width, -1), SHARDS, scatter_dimension=0, tiled=True)
        return mine.astype(F32)

    own_d = owners(grad_in_d, grad_out_d)
    own_t = owners(grad_proj_t, grad_out_t)
    own_s = owners(grad_proj_s, grad_out_s)

    vector_grads = jnp.stack([
        grad_g_s, grad_b_s, grad_ob_s, grad_g_t, grad_b_t, grad_ob_t, grad_g_d, grad_b_d, grad_ob_d,
    ])
    vector_grads = vector_grads.reshape(-1, n_own, strip).transpose(1, 0, 2).reshape(n_own, -1)

    def spread_bias(rows, shape):
        lanes = shape[-1]
        cut = rows.reshape(n_head, -1, n_own, lanes).transpose(0, 2, 1, 3)
        return cut.reshape(n_head, n_own, -1)

    odd_grads = jnp.concatenate([
        spread_bias(sums_s[:, ::2], space_bias.shape),
        spread_bias(sums_t[:, ::2], time_bias.shape),
        spread_bias(grad_bias_d, dense_bias.shape),
    ], axis=2)
    both = jnp.concatenate([vector_grads, odd_grads.transpose(1, 0, 2).reshape(n_own, -1)], axis=1)
    mine = lax.psum_scatter(both, ("clip", "seq"), scatter_dimension=0, tiled=True)
    mine = lax.psum(mine, "head")[0]
    got = [mine[i * strip:(i + 1) * strip] for i in range(9)]
    rest = mine[9 * strip:].reshape(n_head, -1)
    rest = lax.dynamic_index_in_dim(rest, here, axis=0, keepdims=False)
    odd_got = []
    at = 0
    for v in odd:
        odd_got.append(rest[at:at + v.size].reshape(v.shape))
        at += v.size

    def share_rows(rows):
        low = rows.astype(BF).reshape(frames, places, width)
        both_rows = lax.all_gather(low, "head", axis=0, tiled=True)
        return both_rows.astype(F32)[None]

    return (
        share_rows(result),
        share_rows(input_own),
        got[0],
        got[1],
        own_s[:, :3 * part].reshape(space_proj.shape),
        odd_got[0],
        own_s[:, 3 * part:].T,
        got[2],
        got[3],
        got[4],
        own_t[:, :3 * part].reshape(time_proj.shape),
        odd_got[1],
        own_t[:, 3 * part:].T,
        got[5],
        got[6],
        got[7],
        own_d[:, :hidden],
        odd_got[2],
        own_d[:, hidden:].T,
        got[8],
    )


def solution(mesh):
    both = ("clip", "seq")
    rows = P("clip", "seq", None, None)
    vec = P(both)
    weights = (
        vec, vec, P(both, None, "head"), P(None, "head", both), P("head", both), vec,
        vec, vec, P(both, None, "head"), P(None, "head", both), P("head", both), vec,
        vec, vec, P(both, "head"), P("head", both), P("head", both), vec,
    )
    return jax.shard_map(
        body,
        mesh=mesh,
        in_specs=(rows,) + weights + (rows,),
        out_specs=(rows, rows) + weights,
        check_vma=False,
    )
```

time: 1190 us -> 794 us (0.67)
  waiting for transfers between devices: 528 us -> 282 us
  blocking collectives: 249 us -> 109 us
  local copies, waits for them, and re-layouts: 163 us -> 196 us
  other arithmetic: 99.1 us -> 68.5 us
  matrix products: 114 us -> 95.3 us
    psum x5 -> x0, waiting for transfers between devices: 171 us -> none  [head_total(): lax.psum(partial_rows.astype(jnp.bfloat16), 'head').astype(jnp.float32)]
    reduce_scatter x6 -> x3, waiting for transfers between devices: 328 us -> 218 us  [owners(): lax.psum_scatter(both.reshape(n_head * width, -1), SHARDS, scatter_dimens...]
    all_gather x5 -> x1, blocking collectives: 125 us -> 43.6 us  [gather(): return lax.all_gather(block, SHARDS, axis=0, tiled=False)]
    unnamed x2 -> x1, blocking collectives: 125 us -> 60.6 us
    reduce_sum x20 -> x11, other arithmetic: 52.2 us -> 15.3 us  [the longest x1 5.41 us: body(): grad_ob_d = jnp.sum(cot, axis=0)]
    all_gather x4 -> x5, waiting for transfers between devices: 0.58 us -> 32.6 us  [the longest x3 32.6 us: gather(): return lax.all_gather(block, SHARDS, axis=0, tiled=False)]
    concatenate x1 -> x7, local copies, waits for them, and re-layouts: 0.07 us -> 26.6 us  [the longest x3 26.2 us: owners(): both = jnp.concatenate([proj_grad.astype(BF), out_grad.astype(BF)], axis=2)]
    convert_element_type x27 -> x14, local copies, waits for them, and re-layouts: 55.8 us -> 35 us  [the longest x4 21 us: attend_back(): jnp.stack([grad_queries, grad_keys, grad_values], axis=3).astype(BF)]
  transfers between devices with their start and end apart: 19 -> 12, of which waited for: 13 -> 9; matrix products, arithmetic and copies ran while one was open for 15% -> 34% of each run, Pallas kernels for 0% -> 0%
where the time goes in v1:
time: 794 us; the launch traced here: 786 us
  waiting for transfers between devices  282 us (36%)
  local copies, waits for them, and re-layouts  196 us (25%)
  blocking collectives  109 us (14%)
  matrix products  95.3 us (12%)
  other arithmetic  68.5 us (9%)
  starting transfers between devices  18.6 us (2%)
  between operations  15.7 us (2%)
    reduce_scatter x3, waiting for transfers between devices, owners(): lax.psum_scatter(both.reshape(n_head * width, -1), SHARDS, scatter_dimens...  218 us
    dot_general x30, matrix products, product(): return jnp.einsum(form, left, right, preferred_element_type=F32)  95.3 us
    unnamed x1, blocking collectives  60.6 us
    all_gather x1, blocking collectives, gather(): return lax.all_gather(block, SHARDS, axis=0, tiled=False)  43.6 us
    all_gather x3, waiting for transfers between devices, gather(): return lax.all_gather(block, SHARDS, axis=0, tiled=False)  32.6 us
    unnamed x171, local copies, waits for them, and re-layouts  31.3 us
    all_to_all x2, waiting for transfers between devices, to_places(): lax.all_to_all(cut, PLACE_AXES, split_axis=0, concat_axis=0, tiled=True)  26.3 us
    concatenate x3, local copies, waits for them, and re-layouts, owners(): both = jnp.concatenate([proj_grad.astype(BF), out_grad.astype(BF)], axis=2)  26.2 us
  transfers between devices with their start and end apart: 12, of which 9 were waited for; matrix products, arithmetic and copies ran while one was open for 34% of the time, Pallas kernels for 0%

profile of v1, /device:TPU:0, one launch (start us, length us, event | category | flops | bytes accessed | tf_op | source)
XLA Modules:
  0.0 785.8 jit_solution(1498419523730347279)
XLA Ops:
  14.2 43.6 %all-gather.3 = bf16[32,1,624]{2,1,0:T(2,128)(2,1)S(1)} all-gather(bf16[1,1,624]{2,1,0:T(2,128)(2,1)S(1)} %bitcast.436), channel_id=1, replica_groups=mesh['clip'=4,'seq'=4,'head'=2] {'head','clip','seq'}, dimensions={0}, use_global_device_ids=true | all-gather | bytes 41184 | tf_op jit(solution)/shard_map/all_gather | solution.py:91
  59.7 5.4 fusion.140
  69.6 8.6 %all-gather.14.cloned.1.call-done = bf16[1536,1536]{1,0:T(8,128)(2,1)} async-done(((bf16[48,1536]{1,0:T(8,128)(2,1)}), bf16[1536,1536]{1,0:T(8,128)(2,1)}) %all-gather.14.cloned.1.call-update) | async-done | bytes 4718608 | tf_op jit(solution)/shard_map/all_gather | solution.py:91
  78.1 4.9 fusion.52
  83.0 6.9 reshape.664
  90.0 4.9 fusion.147
  96.8 2.6 copy.373
  102.2 4.4 fusion.152
  111.0 2.4 fusion.153
  119.7 4.4 all-to-all-start
  124.1 16.6 %all-to-all-done = bf16[8,2,25,768]{3,1,2,0:T(2,128)(2,1)} async-done(((bf16[8,2,25,768]{3,1,2,0:T(2,128)(2,1)}), bf16[8,2,25,768]{3,1,2,0:T(2,128)(2,1)}, u32[]{:S(2)}, u32[]{:S(2)}) %all-to-all-start) | async-done | bytes 614432 | tf_op jit(solution)/shard_map/all_to_all | solution.py:77
  143.0 2.7 reshape.595
  145.7 4.0 all-gather.16.cloned.1.call-done
  149.7 5.0 fusion.49
  154.7 6.6 reshape_reshape.5
  161.3 3.4 fusion.146
  166.4 10.4 %fusion.154 = (f32[2,25,6,16]{3,2,1,0:T(8,128)S(1)}, f32[2,25,6,16,16]{3,4,2,1,0:T(8,128)S(1)}) fusion(f32[2,25,6,16,16]{3,4,2,1,0:T(8,128)S(1)} %fusion.104), kind=kOutput, calls=%fused_computation.256 | output fusion | flops 307215 | bytes 633600 | tf_op jit(solution)/shard_map/sub | solution.py:52
  179.9 3.4 reshape.599
  183.3 3.0 fusion.77
  186.3 2.6 reshape.601
  191.2 4.4 all-to-all-start.1
  199.6 2.4 copy.312
  202.0 2.5 reshape.606
  204.5 3.8 all-to-all-done.1
  210.9 2.4 reshape.635
  216.2 20.0 %all-gather.18.cloned.1.call-done = bf16[1536,3072]{1,0:T(8,128)(2,1)} async-done(((bf16[48,3072]{1,0:T(8,128)(2,1)}), bf16[1536,3072]{1,0:T(8,128)(2,1)}) %all-gather.18.cloned.1.call-update) | async-done | bytes 9437200 | tf_op jit(solution)/shard_map/all_gather | solution.py:91
  236.2 16.1 %fusion.10 = (bf16[2,392,1536]{2,1,0:T(8,128)(2,1)}, f32[2,392,1536]{2,1,0:T(8,128)S(1)}, f32[2,1536,392]{1,2,0:T(8,128)}) fusion(f32[2,1536]{1,0:T(2,128)S(1)} %add.191, f32[392,768]{1,0:T(8,128)} %copy-done.5, f32[768]{0:T(1024)S(1)} %copy-done.58, f32[768]{0:T(1024)S(1)} %copy-done.52, f32[392]{0:T(512)S(1)} %add_rsqrt_fusion.1, ...), kind=kOutput, calls=%fused_computation.23 | convolution fusion | flops 1930672128 | bytes 17986624 | tf_op jit(solution)/shard_map/nd,hdk->hnk/dot_general | solution.py:15
  252.3 5.9 fusion.155
  258.2 2.4 multiply_reduce_fusion.4
  268.0 4.7 all-to-all-start.2
  272.7 9.7 %all-to-all-done.2 = bf16[8,2,25,768]{3,1,2,0:T(2,128)(2,1)} async-done(((bf16[8,2,25,768]{3,1,2,0:T(2,128)(2,1)}), bf16[8,2,25,768]{3,1,2,0:T(2,128)(2,1)}, u32[]{:S(2)}, u32[]{:S(2)}) %all-to-all-start.2) | async-done | bytes 614432 | tf_op jit(solution)/shard_map/all_to_all | solution.py:77
  284.8 2.7 reshape.609
  287.4 2.9 fusion.90
  290.3 3.0 reshape.611
  293.4 3.8 multiply_reduce_fusion.2
  304.9 3.4 copy.318
  308.3 7.1 convert_element_type.279
  315.4 5.0 fusion.74
  320.4 2.6 reshape.613
  325.3 4.4 all-to-all-start.3
  329.8 6.3 fusion.86
  341.6 2.6 slice_convert_fusion
  344.4 2.6 copy.320
  347.0 2.5 reshape.637
  353.1 2.7 fusion.91
  355.8 3.1 reshape.665
  358.9 2.6 copy.323
  361.5 3.7 fusion.93
  370.3 3.9 copy.328
  374.2 6.6 convert_element_type.289
  380.8 5.3 multiply_reduce_fusion.6
  390.1 3.1 fusion.32
  393.3 2.4 pad_maximum_fusion.2
  395.7 6.7 copy.350
  411.5 2.4 pad_maximum_fusion.1
  413.9 6.7 copy.349
  422.0 4.7 convert_bitcast_fusion
  426.7 3.5 convert_bitcast_fusion.1
  430.2 10.2 %pad_maximum_fusion = bf16[2,768,3072]{1,2,0:T(8,128)(2,1)} fusion(bf16[2,768,1536]{1,2,0:T(8,128)(2,1)S(1)} %convert_bitcast_fusion, bf16[2,768,1536]{1,2,0:T(8,128)(2,1)S(1)} %convert_bitcast_fusion.1), kind=kLoop, calls=%fused_computation.2 | loop fusion | flops 18874368 | bytes 18874368 | tf_op jit(solution)/shard_map/concatenate | solution.py:239
  440.4 12.8 %copy.351 = bf16[2,768,3072]{2,1,0:T(8,128)(2,1)} copy(bf16[2,768,3072]{1,2,0:T(8,128)(2,1)} %pad_maximum_fusion) | data formatting | bytes 18874368 | tf_op jit(solution)/shard_map/concatenate | solution.py:239
  474.0 60.6 %all-reduce.2 = f32[16,816]{1,0:T(8,128)S(1)} all-reduce(f32[16,816]{1,0:T(8,128)S(1)} %pad_maximum_fusion.6), channel_id=5, replica_groups=mesh['clip'=4,'seq'=4,'head'=2] {'clip','seq'}, use_global_device_ids=true, to_apply=%region_30.31.clone | all-reduce | flops 13056 | bytes 104448
  535.2 4.9 psum.7
  554.2 80.1 %reduce-scatter.4.cloned.1.call-done = bf16[48,1536]{1,0:T(8,128)(2,1)} async-done(((bf16[1536,1536]{1,0:T(8,128)(2,1)}), bf16[48,1536]{1,0:T(8,128)(2,1)}) %reduce-scatter.4.cloned.1.call-update) | async-done | bytes 147472 | tf_op jit(solution)/shard_map/reduce_scatter | solution.py:240
  637.5 137.9 %reduce-scatter.8.cloned.1.call-done = bf16[48,3072]{1,0:T(8,128)(2,1)} async-done(((bf16[1536,3072]{1,0:T(8,128)(2,1)}), bf16[48,3072]{1,0:T(8,128)(2,1)}) %reduce-scatter.8.cloned.1.call-update) | async-done | bytes 294928 | tf_op jit(solution)/shard_map/reduce_scatter | solution.py:240
  (371 shorter events, 137.1 us)
Async XLA Ops:
  7.2 5.5 copy-start.42
  7.2 5.6 copy-start.43
  7.2 6.3 copy-start.60
  7.2 6.5 copy-start.61
  7.2 6.5 copy-start.59
  7.2 6.7 copy-start.71
  7.3 6.8 copy-start.62
  7.3 6.8 copy-start.63
  7.3 6.8 copy-start.64
  7.3 6.8 copy-start.65
  7.3 6.8 copy-start.66
  7.3 6.8 copy-start.67
  7.3 6.8 copy-start.68
  7.3 6.8 copy-start.69
  7.3 70.8 %all-gather.14.cloned.1.call-start = ((), (), s32[]{:S(2)}) async-start(), calls=%async_computation.12 | async-start | bytes 4866048 | tf_op jit(solution)/shard_map/all_gather | solution.py:91
  10.1 139.6 %all-gather.16.cloned.1.call-start = ((), (), s32[]{:S(2)}) async-start(), calls=%async_computation.13 | async-start | bytes 4866048 | tf_op jit(solution)/shard_map/all_gather | solution.py:91
  12.7 223.5 %all-gather.18.cloned.1.call-start = ((), (), s32[]{:S(2)}) async-start(), calls=%async_computation.14 | async-start | bytes 9732096 | tf_op jit(solution)/shard_map/all_gather | solution.py:91
  58.8 19.3 %copy-start.44 = (f32[768]{0:T(1024)}, f32[768]{0:T(1024)S(1)}, u32[]{:S(2)}) copy-start(f32[768]{0:T(1024)S(1)} %mul.251) | copy-start | bytes 9220
  58.9 19.3 %copy-start.50 = (f32[768]{0:T(1024)}, f32[768]{0:T(1024)S(1)}, u32[]{:S(2)}) copy-start(f32[768]{0:T(1024)S(1)} %add.166) | copy-start | bytes 9220
  65.1 4.4 copy-start.1
  65.1 2.4 copy-start.34
  65.3 12.8 %copy-start.54 = (f32[392]{0:T(512)}, f32[392]{0:T(512)S(1)}, u32[]{:S(2)}) copy-start(f32[392]{0:T(512)S(1)} %div.57) | copy-start | bytes 4708
  68.1 14.9 %copy-start.56 = (f32[392]{0:T(512)}, f32[392]{0:T(512)S(1)}, u32[]{:S(2)}) copy-start(f32[392]{0:T(512)S(1)} %rsqrt.29) | copy-start | bytes 4708
  102.2 4.4 copy-start.38
  106.6 2.3 copy-start
  113.8 5.9 copy-start.47
  119.7 21.0 %all-to-all-start = ((bf16[8,2,25,768]{3,1,2,0:T(2,128)(2,1)}), bf16[8,2,25,768]{3,1,2,0:T(2,128)(2,1)}, u32[]{:S(2)}, u32[]{:S(2)}) async-start(bf16[8,2,25,768]{3,1,2,0:T(2,128)(2,1)} %bitcast.406), calls=%async_computation | async-start | bytes 1228800 | tf_op jit(solution)/shard_map/all_to_all | solution.py:77
  164.8 12.1 %copy-start.32 = (bf16[2,25,16,1,6,64]{5,4,3,2,1,0:T(8,128)(2,1)}, bf16[2,25,16,1,6,64]{5,4,3,2,1,0:T(8,128)(2,1)S(1)}, u32[]{:S(2)}) copy-start(bf16[2,25,16,1,6,64]{5,4,3,2,1,0:T(8,128)(2,1)S(1)} %get-tuple-element.148) | copy-start | bytes 1843204
  191.2 17.1 %all-to-all-start.1 = ((bf16[8,2,25,768]{3,1,2,0:T(2,128)(2,1)}), bf16[8,2,25,768]{3,1,2,0:T(2,128)(2,1)}, u32[]{:S(2)}, u32[]{:S(2)}) async-start(bf16[8,2,25,768]{3,1,2,0:T(2,128)(2,1)} %copy.308), calls=%async_computation.1 | async-start | bytes 1228800 | tf_op jit(solution)/shard_map/all_to_all | solution.py:85
  209.8 3.6 copy-start.53
  213.3 22.9 %copy-start.52 = (f32[768]{0:T(1024)S(1)}, f32[768]{0:T(1024)}, u32[]{:S(2)}) copy-start(f32[768]{0:T(1024)} %mul.267) | copy-start | bytes 9220
  213.3 22.9 %copy-start.58 = (f32[768]{0:T(1024)S(1)}, f32[768]{0:T(1024)}, u32[]{:S(2)}) copy-start(f32[768]{0:T(1024)} %add.188) | copy-start | bytes 9220
  236.2 16.1 %copy-start.23 = (f32[392,768]{1,0:T(8,128)S(1)}, f32[392,768]{1,0:T(8,128)}, u32[]{:S(2)}) copy-start(f32[392,768]{1,0:T(8,128)} %reshape.606) | copy-start | bytes 3612676
  236.2 16.1 %copy-start.70 = (bf16[1536,3072]{1,0:T(8,128)(2,1)S(1)}, bf16[1536,3072]{1,0:T(8,128)(2,1)}, u32[]{:S(2)}) copy-start(bf16[1536,3072]{1,0:T(8,128)(2,1)} %all-gather.18.cloned.1.call-done) | copy-start | bytes 28311556
  252.3 5.9 copy-start.6
  258.2 2.4 copy-start.73
  263.1 9.6 %copy-start.46 = (f32[1,16,48]{2,1,0:T(8,128)S(1)}, f32[1,16,48]{2,1,0:T(8,128)}, u32[]{:S(2)}) copy-start(f32[1,16,48]{2,1,0:T(8,128)} %get-tuple-element.152) | copy-start | bytes 9220
  268.0 14.5 %all-to-all-start.2 = ((bf16[8,2,25,768]{3,1,2,0:T(2,128)(2,1)}), bf16[8,2,25,768]{3,1,2,0:T(2,128)(2,1)}, u32[]{:S(2)}, u32[]{:S(2)}) async-start(bf16[8,2,25,768]{3,1,2,0:T(2,128)(2,1)} %bitcast.405), calls=%async_computation.2 | async-start | bytes 1228800 | tf_op jit(solution)/shard_map/all_to_all | solution.py:77
  293.4 3.8 copy-start.17
  293.4 3.9 copy-start.33
  298.1 5.8 copy-start.22
  325.3 14.2 %all-to-all-start.3 = ((bf16[8,2,25,768]{3,1,2,0:T(2,128)(2,1)}), bf16[8,2,25,768]{3,1,2,0:T(2,128)(2,1)}, u32[]{:S(2)}, u32[]{:S(2)}) async-start(bf16[8,2,25,768]{3,1,2,0:T(2,128)(2,1)} %copy.319), calls=%async_computation.3 | async-start | bytes 1228800 | tf_op jit(solution)/shard_map/all_to_all | solution.py:85
  329.7 213.5 %all-gather.10.cloned.1.call-start = ((), (), s32[]{:S(2)}) async-start(), calls=%async_computation.7 | async-start | bytes 1843200 | tf_op jit(solution)/shard_map/all_gather | solution.py:276
  338.1 209.0 %all-gather.12.cloned.1.call-start = ((), (), s32[]{:S(2)}) async-start(), calls=%async_computation.8 | async-start | bytes 1843200 | tf_op jit(solution)/shard_map/all_gather | solution.py:276
  344.4 5.1 copy-start.48
  355.8 9.4 %slice-start = ((s8[4915200]{0:T(1024)(128)(4,1)}), s8[720896]{0:T(1024)(128)(4,1)S(1)}, s32[]{:S(2)}) async-start(s8[4915200]{0:T(1024)(128)(4,1)} %bitcast.393), calls=%async_computation.15 | async-start | bytes 1441792
  361.5 3.9 slice-start.1
  361.5 4.1 copy-start.39
  361.5 4.3 copy-start.40
  365.8 3.6 copy-start.26
  374.2 6.6 copy-start.45
  374.2 6.6 copy-start.55
  374.2 6.6 copy-start.57
  380.8 5.3 copy-start.9
  387.5 2.6 copy-start.31
  387.5 163.4 %reduce-scatter.6.cloned.1.call-start = ((), (), s32[]{:S(2)}) async-start(), calls=%async_computation.10 | async-start | bytes 4866048 | tf_op jit(solution)/shard_map/reduce_scatter | solution.py:240
  402.4 5.3 copy-start.10
  402.4 231.9 %reduce-scatter.4.cloned.1.call-start = ((), (), s32[]{:S(2)}) async-start(), calls=%async_computation.9 | async-start | bytes 4866048 | tf_op jit(solution)/shard_map/reduce_scatter | solution.py:240
  404.8 2.9 copy-start.25
  420.7 6.0 copy-start.7
  420.7 354.6 %reduce-scatter.8.cloned.1.call-start = ((), (), s32[]{:S(2)}) async-start(), calls=%async_computation.11 | async-start | bytes 9732096 | tf_op jit(solution)/shard_map/reduce_scatter | solution.py:240
  422.0 4.7 copy-start.74
  464.8 4.3 copy-start.21
  469.9 2.6 copy-start.28
  (25 other events, 33.6 us)
Sparse Core Ops, SparseCore 0:
  11.6 66.4 all-gather.13
  81.6 68.0 all-gather.15
  153.2 83.0 all-gather.17
  338.2 23.0 all-gather.9
  387.7 21.6 all-gather.11
  414.7 107.4 reduce-scatter.5
  527.7 106.4 reduce-scatter.3
  640.2 135.1 reduce-scatter.7

commit v2 on v1

--- a/solution.py
+++ b/solution.py
@@ -1,7 +1,12 @@
+import functools
+
 import jax
 import jax.numpy as jnp
 from jax import lax
+from jax.experimental import pallas as pl
+from jax.experimental.pallas import tpu as pltpu
 from jax.sharding import PartitionSpec as P
+
 
 HEAD_DIM = 64
 NORM_EPS = 1e-06
@@ -9,6 +14,195 @@
 F32 = jnp.float32
 SHARDS = ("head", "clip", "seq")
 PLACE_AXES = ("seq", "head")
+
+MESH = pl.DeviceIdType.MESH
+
+
+def position():
+    seq = lax.axis_index("seq")
+    return lax.axis_index("clip"), seq // 2, lax.rem(seq, 2), lax.axis_index("head")
+
+
+def greet(n_clip, clip, side, core, head):
+    barrier = pltpu.get_barrier_semaphore()
+    peers = [{"seq": side * 2 + 1 - core}, {"seq": (1 - side) * 2 + core}, {"head": 1 - head}]
+    for step in range(1, n_clip):
+        peers.append({"clip": lax.rem(clip + step, n_clip)})
+    for peer in peers:
+        pl.semaphore_signal(barrier, inc=1, device_id=peer, device_id_type=MESH)
+    pl.semaphore_wait(barrier, len(peers))
+
+
+def scatter_kernel(n_clip, pieces, n_src, *refs):
+    srcs, outs, scratch = refs[:n_src], refs[n_src:n_src + 2], refs[n_src + 2:]
+    kinds = (scratch[0:5], scratch[5:10])
+    sems = scratch[10]
+    clip, side, core, head = position()
+    greet(n_clip, clip, side, core, head)
+
+    def send(src, dst, piece, kind, peer):
+        return pltpu.make_async_remote_copy(
+            src_ref=src, dst_ref=dst, send_sem=sems.at[0, piece, kind],
+            recv_sem=sems.at[1, piece, kind], device_id=peer, device_id_type=MESH,
+        )
+
+    started = []
+    firsts = []
+    for i, (kind, slot, src, at, size, _) in enumerate(pieces):
+        own, got = kinds[kind][0], kinds[kind][1]
+        cols = pl.ds(at, size)
+        pairs = []
+        for b in range(2):
+            away = send(
+                srcs[src].at[:, :, b, 1 - core, :, cols], got.at[slot, :, b], i, b,
+                {"seq": side * 2 + 1 - core},
+            )
+            away.start()
+            near = pltpu.make_async_copy(
+                srcs[src].at[:, :, b, core, :, cols], own.at[slot, :, b],
+                sems.at[0, i, n_clip + 3 + b],
+            )
+            near.start()
+            started.append(away)
+            pairs.append((away, near))
+        firsts.append(pairs)
+
+    seconds, thirds, fourths = {}, {}, {}
+
+    def add_into(own, got, dtype):
+        own[...] = (own[...].astype(F32) + got[...].astype(F32)).astype(dtype)
+
+    def first(i):
+        kind, slot = pieces[i][:2]
+        own, got, mid = kinds[kind][:3]
+        for away, near in firsts[i]:
+            near.wait()
+            away.wait_recv()
+        dtype = own.dtype
+
+        def step(c, carry):
+            for a in range(2):
+                for b in range(2):
+                    add_into(own.at[slot, a, b, c], got.at[slot, a, b, c], dtype)
+            return carry
+
+        lax.fori_loop(0, n_clip, step, 0)
+        if i % 2 == 0:
+            away = send(own.at[slot, 1 - head], mid.at[slot], i, 2, {"head": 1 - head})
+        else:
+            away = send(
+                own.at[slot, :, 1 - side], mid.at[slot], i, 2,
+                {"seq": (1 - side) * 2 + core},
+            )
+        away.start()
+        started.append(away)
+        seconds[i] = away
+
+    def second(i):
+        kind, slot = pieces[i][:2]
+        own, _, mid, late = kinds[kind][:4]
+        seconds[i].wait_recv()
+        dtype = own.dtype
+        if i % 2 == 0:
+            def step(c, carry):
+                for b in range(2):
+                    add_into(own.at[slot, head, b, c], mid.at[slot, b, c], dtype)
+                return carry
+
+            lax.fori_loop(0, n_clip, step, 0)
+            away = send(
+                own.at[slot, head, 1 - side], late.at[slot], i, 3,
+                {"seq": (1 - side) * 2 + core},
+            )
+        else:
+            def step(c, carry):
+                for a in range(2):
+                    add_into(own.at[slot, a, side, c], mid.at[slot, a, c], dtype)
+                return carry
+
+            lax.fori_loop(0, n_clip, step, 0)
+            away = send(own.at[slot, 1 - head, side], late.at[slot], i, 3, {"head": 1 - head})
+        away.start()
+        started.append(away)
+        thirds[i] = away
+
+    def third(i):
+        kind, slot = pieces[i][:2]
+        own, _, _, late, last = kinds[kind]
+        thirds[i].wait_recv()
+        dtype = own.dtype
+
+        def step(c, carry):
+            add_into(own.at[slot, head, side, c], late.at[slot, c], dtype)
+            return carry
+
+        lax.fori_loop(0, n_clip, step, 0)
+        fourths[i] = []
+        for d in range(1, n_clip):
+            there = lax.rem(clip + d, n_clip)
+            away = send(
+                own.at[slot, head, side, there], last.at[slot, d - 1], i, 3 + d, {"clip": there}
+            )
+            away.start()
+            started.append(away)
+            fourths[i].append(away)
+
+    def fourth(i):
+        kind, slot, _, _, size, out_at = pieces[i]
+        own, last = kinds[kind][0], kinds[kind][4]
+        total = own[slot, head, side, clip].astype(F32)
+        for d in range(1, n_clip):
+            fourths[i][d - 1].wait_recv()
+            total = total + last[slot, d - 1].astype(F32)
+        outs[kind][:, out_at:out_at + size] = total
+
+    steps = (first, second, third, fourth)
+    for wave in range(len(pieces) + 3):
+        for back, stage in enumerate(steps):
+            if 0 <= wave - back < len(pieces):
+                stage(wave - back)
+    for away in started:
+        away.wait_send()
+
+
+def scatter_grads(grads, vectors, name_id):
+    n_head, n_clip, sides, _, strip, _ = grads[0].shape
+    pieces = [(1, 0, len(grads), 0, vectors.shape[5], 0)]
+    chunk = min(g.shape[5] for g in grads)
+    at_out = 0
+    for j, g in enumerate(grads):
+        for at in range(0, g.shape[5], chunk):
+            pieces.append((0, len(pieces) - 1, j, at, chunk, at_out))
+            at_out += chunk
+    n_low = len(pieces) - 1
+
+    def buffers(n, rows, cols, dtype):
+        return [
+            pltpu.VMEM((n, n_head, sides, n_clip, rows, cols), dtype),
+            pltpu.VMEM((n, n_head, sides, n_clip, rows, cols), dtype),
+            pltpu.VMEM((n, 2, n_clip, rows, cols), dtype),
+            pltpu.VMEM((n, n_clip, rows, cols), dtype),
+            pltpu.VMEM((n, n_clip - 1, rows, cols), dtype),
+        ]
+
+    any_spec = pl.BlockSpec(memory_space=pl.ANY)
+    vmem = pl.BlockSpec(memory_space=pltpu.VMEM)
+    n_src = len(grads) + 1
+    return pl.pallas_call(
+        functools.partial(scatter_kernel, n_clip, tuple(pieces), n_src),
+        out_shape=(
+            jax.ShapeDtypeStruct((strip, at_out), F32),
+            jax.ShapeDtypeStruct(vectors.shape[4:], F32),
+        ),
+        in_specs=[any_spec] * n_src,
+        out_specs=(vmem, vmem),
+        scratch_shapes=buffers(n_low, strip, chunk, BF) + buffers(1, *vectors.shape[4:], F32)
+        + [pltpu.SemaphoreType.DMA((2, len(pieces), n_clip + 5))],
+        compiler_params=pltpu.CompilerParams(
+            collective_id=name_id, has_side_effects=True, vmem_limit_bytes=40 * 1024 * 1024
+        ),
+        name="scatter_grads",
+    )(*grads, vectors)
 
 
 def product(form, left, right):
@@ -208,6 +402,8 @@
     grad_normed = product("hnk,hdk->nd", low_pre, in_d)
     grad_v, grad_g_d, grad_b_d = norm_back(unit_d, rate_d, g_d, grad_normed)
     stream_t = cot + grad_v
+    dense_grads = jnp.concatenate([grad_in_d.astype(BF), grad_out_d.astype(BF)], axis=2)
+    stream_t, dense_grads = lax.optimization_barrier((stream_t, dense_grads))
 
     grad_ob_t = jnp.sum(stream_t, axis=0)
     low_t = to_places(stream_t.astype(BF).reshape(frames, places, width), count)
@@ -235,40 +431,52 @@
     grad_v, grad_g_s, grad_b_s = norm_back(unit_s, rate_s, g_s, grad_rows)
     input_own = stream_s + grad_v
 
-    def owners(proj_grad, out_grad):
-        both = jnp.concatenate([proj_grad.astype(BF), out_grad.astype(BF)], axis=2)
-        mine = lax.psum_scatter(both.reshape(n_head * width, -1), SHARDS, scatter_dimension=0, tiled=True)
-        return mine.astype(F32)
-
-    own_d = owners(grad_in_d, grad_out_d)
-    own_t = owners(grad_proj_t, grad_out_t)
-    own_s = owners(grad_proj_s, grad_out_s)
-
     vector_grads = jnp.stack([
         grad_g_s, grad_b_s, grad_ob_s, grad_g_t, grad_b_t, grad_ob_t, grad_g_d, grad_b_d, grad_ob_d,
     ])
-    vector_grads = vector_grads.reshape(-1, n_own, strip).transpose(1, 0, 2).reshape(n_own, -1)
+    vector_grads = vector_grads.reshape(-1, n_own, strip).transpose(1, 0, 2).reshape(1, n_own, -1)
 
     def spread_bias(rows, shape):
         lanes = shape[-1]
         cut = rows.reshape(n_head, -1, n_own, lanes).transpose(0, 2, 1, 3)
         return cut.reshape(n_head, n_own, -1)
 
-    odd_grads = jnp.concatenate([
+    small_grads = jnp.concatenate([
+        jnp.broadcast_to(vector_grads, (n_head,) + vector_grads.shape[1:]),
         spread_bias(sums_s[:, ::2], space_bias.shape),
         spread_bias(sums_t[:, ::2], time_bias.shape),
         spread_bias(grad_bias_d, dense_bias.shape),
     ], axis=2)
-    both = jnp.concatenate([vector_grads, odd_grads.transpose(1, 0, 2).reshape(n_own, -1)], axis=1)
-    mine = lax.psum_scatter(both, ("clip", "seq"), scatter_dimension=0, tiled=True)
-    mine = lax.psum(mine, "head")[0]
+
+    def owners(grad):
+        mine = lax.psum_scatter(
+            grad.astype(BF).reshape(n_head * width, -1), SHARDS, scatter_dimension=0, tiled=True
+        )
+        return mine.astype(F32)
+
+    own_d = owners(dense_grads)
+    if strip % 16 == 0:
+        blocks = (n_head, lax.axis_size("clip"), 2, 2)
+        low = [
+            g.astype(BF).reshape(blocks + (strip, -1))
+            for g in (grad_proj_s, grad_out_s, grad_proj_t, grad_out_t)
+        ]
+        room = -small_grads.shape[2] % 1024
+        tiles = jnp.pad(small_grads, ((0, 0), (0, 0), (0, room))).reshape(blocks + (-1, 128))
+        large, mine = scatter_grads(low, tiles, 1)
+        mine = mine.reshape(-1)
+        step = 4 * part
+        own_s, own_t = large[:, :step], large[:, step:]
+    else:
+        own_s = owners(jnp.concatenate([grad_proj_s, grad_out_s], axis=2))
+        own_t = owners(jnp.concatenate([grad_proj_t, grad_out_t], axis=2))
+        mine = lax.psum_scatter(small_grads, ("clip", "seq"), scatter_dimension=1, tiled=True)
+        mine = lax.dynamic_index_in_dim(lax.psum(mine, "head"), here, axis=0, keepdims=False)[0]
     got = [mine[i * strip:(i + 1) * strip] for i in range(9)]
-    rest = mine[9 * strip:].reshape(n_head, -1)
-    rest = lax.dynamic_index_in_dim(rest, here, axis=0, keepdims=False)
     odd_got = []
-    at = 0
+    at = 9 * strip
     for v in odd:
-        odd_got.append(rest[at:at + v.size].reshape(v.shape))
+        odd_got.append(mine[at:at + v.size].reshape(v.shape))
         at += v.size
 
     def share_rows(rows):
@@ -309,6 +517,7 @@
         vec, vec, P(both, None, "head"), P(None, "head", both), P("head", both), vec,
         vec, vec, P(both, "head"), P("head", both), P("head", both), vec,
     )
+
     return jax.shard_map(
         body,
         mesh=mesh,

time: 794 us -> 596 us (0.75)
  waiting for transfers between devices: 282 us -> 104 us
  Pallas kernels: 0 us -> 80 us
  blocking collectives: 109 us -> 43.6 us
  local copies, waits for them, and re-layouts: 196 us -> 170 us
  other arithmetic: 68.5 us -> 59.8 us
    reduce_scatter x3 -> x1, waiting for transfers between devices: 218 us -> 31.8 us  [owners(): lax.psum_scatter(grad.astype(BF).reshape(n_head * width, -1), SHARDS, sca...]
    pallas_call x0 -> x1, Pallas kernels: none -> 80 us  [scatter_grads(): pl.pallas_call(functools.partial(scatter_kernel, n_clip, tuple(pieces), n...]
    unnamed x1 -> x0, blocking collectives: 60.6 us -> none
    concatenate x3 -> x0, local copies, waits for them, and re-layouts: 26.2 us -> none  [owners(): both = jnp.concatenate([proj_grad.astype(BF), out_grad.astype(BF)], axis=2)]
    optimization_barrier x0 -> x1, local copies, waits for them, and re-layouts: none -> 12.8 us  [body(): stream_t, dense_grads = lax.optimization_barrier((stream_t, dense_grads))]
    unnamed x171 -> x158, local copies, waits for them, and re-layouts: 31.3 us -> 25.3 us
  transfers between devices with their start and end apart: 12 -> 10, of which waited for: 9 -> 8; matrix products, arithmetic and copies ran while one was open for 34% -> 39% of each run, Pallas kernels for 0% -> 14%
where the time goes in v2:
time: 596 us; the launch traced here: 588 us
  local copies, waits for them, and re-layouts  170 us (29%)
  waiting for transfers between devices  104 us (17%)
  matrix products  100 us (17%)
  Pallas kernels  80 us (13%)
  other arithmetic  59.8 us (10%)
  blocking collectives  43.6 us (7%)
  between operations  15.7 us (3%)
  starting transfers between devices  15.5 us (3%)
    dot_general x30, matrix products, product(): return jnp.einsum(form, left, right, preferred_element_type=F32)  100 us
    pallas_call x1, Pallas kernels, scatter_grads(): pl.pallas_call(functools.partial(scatter_kernel, n_clip, tuple(pieces), n...  80 us
    all_gather x1, blocking collectives, gather(): return lax.all_gather(block, SHARDS, axis=0, tiled=False)  43.6 us
    all_gather x3, waiting for transfers between devices, gather(): return lax.all_gather(block, SHARDS, axis=0, tiled=False)  40.5 us
    reduce_scatter x1, waiting for transfers between devices, owners(): lax.psum_scatter(grad.astype(BF).reshape(n_head * width, -1), SHARDS, sca...  31.8 us
    all_to_all x2, waiting for transfers between devices, to_places(): lax.all_to_all(cut, PLACE_AXES, split_axis=0, concat_axis=0, tiled=True)  26.2 us
    unnamed x158, local copies, waits for them, and re-layouts  25.3 us
    convert_element_type x4, local copies, waits for them, and re-layouts, attend_back(): jnp.stack([grad_queries, grad_keys, grad_values], axis=3).astype(BF)  21 us
  transfers between devices with their start and end apart: 10, of which 8 were waited for; matrix products, arithmetic and copies ran while one was open for 39% of the time, Pallas kernels for 14%

profile of v2, /device:TPU:0, one launch (start us, length us, event | category | flops | bytes accessed | tf_op | source)
XLA Modules:
  0.0 588.3 jit_solution(4165542944350706723)
XLA Ops:
  14.2 43.6 %all-gather.3 = bf16[32,1,624]{2,1,0:T(2,128)(2,1)S(1)} all-gather(bf16[1,1,624]{2,1,0:T(2,128)(2,1)S(1)} %bitcast.430), channel_id=1, replica_groups=mesh['clip'=4,'seq'=4,'head'=2] {'head','clip','seq'}, dimensions={0}, use_global_device_ids=true | all-gather | bytes 41184 | tf_op jit(solution)/shard_map/all_gather | solution.py:285
  59.2 5.4 fusion.137
  68.5 9.7 %all-gather.14.cloned.1.call-done = bf16[1536,1536]{1,0:T(8,128)(2,1)} async-done(((bf16[48,1536]{1,0:T(8,128)(2,1)}), bf16[1536,1536]{1,0:T(8,128)(2,1)}) %all-gather.14.cloned.1.call-update) | async-done | bytes 4718608 | tf_op jit(solution)/shard_map/all_gather | solution.py:285
  78.1 4.9 fusion.50
  83.0 6.6 %reshape.651 = bf16[2,2,196,3,6,64]{5,4,3,2,1,0:T(8,128)(2,1)} reshape(bf16[2,392,1152]{2,1,0:T(8,128)(2,1)} %fusion.50) | data formatting | bytes 3612672 | tf_op jit(solution)/shard_map/reshape;reshape | solution.py:239
  89.6 4.9 fusion.143
  96.5 2.9 copy.379
  99.4 2.6 copy.381
  102.0 2.0 fusion.108
  104.0 4.4 fusion.150
  112.7 2.5 fusion.151
  119.5 3.8 all-to-all-start
  123.3 16.5 %all-to-all-done = bf16[8,2,25,768]{3,1,2,0:T(2,128)(2,1)S(1)} async-done(((bf16[8,2,25,768]{3,1,2,0:T(2,128)(2,1)}), bf16[8,2,25,768]{3,1,2,0:T(2,128)(2,1)S(1)}, u32[]{:S(2)}, u32[]{:S(2)}) %all-to-all-start) | async-done | bytes 614432 | tf_op jit(solution)/shard_map/all_to_all | solution.py:271
  141.0 2.0 reshape.583
  143.1 7.3 %all-gather.16.cloned.1.call-done = bf16[1536,1536]{1,0:T(8,128)(2,1)} async-done(((bf16[48,1536]{1,0:T(8,128)(2,1)}), bf16[1536,1536]{1,0:T(8,128)(2,1)}) %all-gather.16.cloned.1.call-update) | async-done | bytes 4718608 | tf_op jit(solution)/shard_map/all_gather | solution.py:285
  150.4 4.9 fusion.47
  155.3 6.6 %reshape_reshape.5 = bf16[2,25,16,3,6,64]{5,4,3,2,1,0:T(8,128)(2,1)} reshape(bf16[2,400,1152]{2,1,0:T(8,128)(2,1)} %fusion.47) | data formatting | bytes 3686400 | tf_op jit(solution)/shard_map/reshape;reshape | solution.py:239
  161.9 3.4 fusion.142
  167.0 10.4 %fusion.152 = (f32[2,25,6,16]{3,2,1,0:T(8,128)S(1)}, f32[2,25,6,16,16]{3,4,2,1,0:T(8,128)S(1)}) fusion(f32[2,25,6,16,16]{3,4,2,1,0:T(8,128)S(1)} %fusion.102), kind=kOutput, calls=%fused_computation.240 | output fusion | flops 307215 | bytes 633600 | tf_op jit(solution)/shard_map/sub | solution.py:246
  180.5 2.7 reshape.587
  183.2 3.0 fusion.75
  189.4 4.0 all-to-all-start.1
  194.1 2.4 copy.319
  196.5 2.4 reshape.594
  198.9 4.4 all-to-all-done.1
  204.8 2.4 reshape.623
  210.1 23.5 %all-gather.18.cloned.1.call-done = bf16[1536,3072]{1,0:T(8,128)(2,1)} async-done(((bf16[48,3072]{1,0:T(8,128)(2,1)}), bf16[1536,3072]{1,0:T(8,128)(2,1)}) %all-gather.18.cloned.1.call-update) | async-done | bytes 9437200 | tf_op jit(solution)/shard_map/all_gather | solution.py:285
  233.6 15.7 %fusion.10 = (bf16[2,392,1536]{2,1,0:T(8,128)(2,1)S(1)}, f32[2,392,1536]{2,1,0:T(8,128)S(1)}, f32[2,1536,392]{1,2,0:T(8,128)}) fusion(f32[2,1536]{1,0:T(2,128)S(1)} %add.181, f32[392,768]{1,0:T(8,128)} %copy-done.9, f32[768]{0:T(1024)S(1)} %add.178, f32[768]{0:T(1024)S(1)} %mul.267, f32[392]{0:T(512)S(1)} %add_rsqrt_fusion.1, ...), kind=kOutput, calls=%fused_computation.23 | convolution fusion | flops 1930672128 | bytes 17986624 | tf_op jit(solution)/shard_map/nd,hdk->hnk/dot_general | solution.py:209
  249.3 6.7 %fusion.153 = (f32[2,1536]{1,0:T(2,128)S(1)}, bf16[2,392,1536]{2,1,0:T(8,128)(2,1)S(1)}) fusion(f32[2,392,1536]{2,1,0:T(8,128)S(1)} %get-tuple-element.145, f32[392,768]{1,0:T(8,128)S(1)} %copy-done.25, bf16[2,768,3072]{2,1,0:T(8,128)(2,1)S(1)} %bitcast.435, f32[2,1536,392]{1,2,0:T(8,128)} %get-tuple-element.195, f32[2,1536]{1,0:T(2,128)S(1)} %add.181), kind=kOutput, calls=%fused_computation.241 | convolution fusion | flops 1871662080 | bytes 17989632 | tf_op jit(solution)/shard_map/nd,hdk->hnk/dot_general | solution.py:209
  256.0 2.4 multiply_reduce_fusion.4
  258.4 3.5 convert_bitcast_fusion.1
  262.0 3.1 convert_bitcast_fusion
  265.1 10.1 %pad_maximum_fusion = bf16[2,768,3072]{1,2,0:T(8,128)(2,1)} fusion(bf16[2,768,1536]{1,2,0:T(8,128)(2,1)S(1)} %convert_bitcast_fusion, bf16[2,768,1536]{1,2,0:T(8,128)(2,1)S(1)} %convert_bitcast_fusion.1), kind=kLoop, calls=%fused_computation.2 | loop fusion | flops 18874368 | bytes 18874368 | tf_op jit(solution)/shard_map/concatenate | solution.py:405
  280.5 3.5 all-to-all-start.2
  284.1 9.7 %all-to-all-done.2 = bf16[8,2,25,768]{3,1,2,0:T(2,128)(2,1)S(1)} async-done(((bf16[8,2,25,768]{3,1,2,0:T(2,128)(2,1)}), bf16[8,2,25,768]{3,1,2,0:T(2,128)(2,1)S(1)}, u32[]{:S(2)}, u32[]{:S(2)}) %all-to-all-start.2) | async-done | bytes 614432 | tf_op jit(solution)/shard_map/all_to_all | solution.py:271
  295.1 2.0 reshape.597
  297.1 3.0 fusion.88
  300.1 3.0 reshape.599
  303.1 3.8 multiply_reduce_fusion.2
  314.7 3.5 copy.325
  318.2 7.1 %convert_element_type.279 = bf16[2,400,1152]{2,1,0:T(8,128)(2,1)} reshape(bf16[2,25,16,3,6,64]{5,4,3,2,1,0:T(8,128)(2,1)} %copy.325) | data formatting | bytes 3686400 | tf_op jit(solution)/shard_map/convert_element_type | solution.py:262
  325.3 5.0 fusion.72
  333.4 3.5 all-to-all-start.3
  337.4 6.6 %fusion.84 = bf16[392,768]{1,0:T(8,128)(2,1)} fusion(f32[392,768]{1,0:T(8,128)} %copy-done.9, bf16[2,392,1536]{2,1,0:T(8,128)(2,1)} %copy-done.68, bf16[2,768,3072]{2,1,0:T(8,128)(2,1)} %bitcast.434, f32[768]{0:T(1024)S(1)} %add.185), kind=kOutput, calls=%fused_computation.104 | convolution fusion | flops 1850591232 | bytes 8936448 | tf_op jit(solution)/shard_map/hnk,hdk->nd/dot_general | solution.py:209
  344.0 2.0 reshape.593
  349.4 2.4 copy.327
  351.8 2.5 reshape.625
  357.8 2.0 fusion.89
  361.6 2.6 copy.330
  364.3 3.7 fusion.91
  373.4 3.9 copy.335
  377.3 6.6 %convert_element_type.289 = bf16[2,392,1152]{1,2,0:T(8,128)(2,1)} reshape(bf16[2,2,196,3,6,64]{2,1,5,4,3,0:T(2,128)(2,1)} %copy.335) | data formatting | bytes 3612672 | tf_op jit(solution)/shard_map/convert_element_type | solution.py:262
  383.8 5.3 multiply_reduce_fusion.6
  390.6 12.8 %copy.357 = bf16[2,768,3072]{2,1,0:T(8,128)(2,1)} copy(bf16[2,768,3072]{1,2,0:T(8,128)(2,1)} %pad_maximum_fusion) | data formatting | bytes 18874368 | tf_op jit(solution)/shard_map/optimization_barrier | solution.py:406
  421.6 5.7 convolution_convert_fusion
  432.9 3.3 stack.98
  436.2 2.8 copy.344
  439.1 3.4 stack.97
  444.2 2.5 stack.96
  449.5 4.1 convolution_convert_fusion.1
  453.6 80.0 %scatter_grads.1 = (f32[48,3072]{1,0:T(8,128)S(1)}, f32[8,128]{1,0:T(8,128)S(1)}) custom-call(bf16[2,4,2,2,48,1152]{5,4,3,2,1,0:T(8,128)(2,1)S(1)} %bitcast.381, bf16[2,4,2,2,48,384]{5,4,3,2,1,0:T(8,128)(2,1)S(1)} %bitcast.379, bf16[2,4,2,2,48,1152]{5,4,3,2,1,0:T(8,128)(2,1)S(1)} %bitcast.380, bf16[2,4,2,2,48,384]{5,4,3,2,1,0:T(8,128)(2,1)S(1)} %bitcast.378, ...), custom_call_target="tpu_custom_call" | custom-call | tf_op jit(solution)/shard_map/scatter_grads/pallas_call | solution.py:191
  539.9 2.4 copy.358
  543.7 2.4 copy.359
  546.1 31.8 %reduce-scatter.2.cloned.1.call-done = bf16[48,3072]{1,0:T(8,128)(2,1)} async-done(((bf16[1536,3072]{1,0:T(8,128)(2,1)}), bf16[48,3072]{1,0:T(8,128)(2,1)}) %reduce-scatter.2.cloned.1.call-update) | async-done | bytes 294928 | tf_op jit(solution)/shard_map/reduce_scatter | solution.py:452
  (340 shorter events, 109.1 us)
Async XLA Ops:
  7.2 5.5 copy-start.42
  7.2 5.6 copy-start.43
  7.2 6.3 %copy-start.56 = (f32[2,3,8]{2,0,1:T(2,128)S(1)}, f32[2,3,8]{2,0,1:T(2,128)}, u32[]{:S(2)}) copy-start(f32[2,3,8]{2,0,1:T(2,128)} %param.24) | copy-start | bytes 580
  7.2 6.5 %copy-start.57 = (f32[2,3,8]{2,0,1:T(2,128)S(1)}, f32[2,3,8]{2,0,1:T(2,128)}, u32[]{:S(2)}) copy-start(f32[2,3,8]{2,0,1:T(2,128)} %param.30) | copy-start | bytes 580
  7.2 6.5 %copy-start.55 = (f32[12,8]{0,1:T(8,128)S(1)}, f32[12,8]{0,1:T(8,128)}, u32[]{:S(2)}) copy-start(f32[12,8]{0,1:T(8,128)} %param.36) | copy-start | bytes 1156
  7.2 6.7 %copy-start.67 = (f32[48]{0:T(128)S(1)}, f32[48]{0:T(128)}, u32[]{:S(2)}) copy-start(f32[48]{0:T(128)} %param.21) | copy-start | bytes 580
  7.3 6.8 %copy-start.58 = (f32[48]{0:T(128)S(1)}, f32[48]{0:T(128)}, u32[]{:S(2)}) copy-start(f32[48]{0:T(128)} %param.26) | copy-start | bytes 580
  7.3 6.8 %copy-start.59 = (f32[48]{0:T(128)S(1)}, f32[48]{0:T(128)}, u32[]{:S(2)}) copy-start(f32[48]{0:T(128)} %param.22) | copy-start | bytes 580
  7.3 6.8 %copy-start.60 = (f32[48]{0:T(128)S(1)}, f32[48]{0:T(128)}, u32[]{:S(2)}) copy-start(f32[48]{0:T(128)} %param.28) | copy-start | bytes 580
  7.3 6.8 %copy-start.61 = (f32[48]{0:T(128)S(1)}, f32[48]{0:T(128)}, u32[]{:S(2)}) copy-start(f32[48]{0:T(128)} %param.27) | copy-start | bytes 580
  7.3 6.8 %copy-start.62 = (f32[48]{0:T(128)S(1)}, f32[48]{0:T(128)}, u32[]{:S(2)}) copy-start(f32[48]{0:T(128)} %param.33) | copy-start | bytes 580
  7.3 6.8 %copy-start.63 = (f32[48]{0:T(128)S(1)}, f32[48]{0:T(128)}, u32[]{:S(2)}) copy-start(f32[48]{0:T(128)} %param.32) | copy-start | bytes 580
  7.3 6.8 %copy-start.64 = (f32[48]{0:T(128)S(1)}, f32[48]{0:T(128)}, u32[]{:S(2)}) copy-start(f32[48]{0:T(128)} %param.38) | copy-start | bytes 580
  7.3 6.8 %copy-start.65 = (f32[48]{0:T(128)S(1)}, f32[48]{0:T(128)}, u32[]{:S(2)}) copy-start(f32[48]{0:T(128)} %param.34) | copy-start | bytes 580
  7.3 70.8 %all-gather.14.cloned.1.call-start = ((), (), s32[]{:S(2)}) async-start(), calls=%async_computation.8 | async-start | bytes 4866048 | tf_op jit(solution)/shard_map/all_gather | solution.py:285
  10.1 140.3 %all-gather.16.cloned.1.call-start = ((), (), s32[]{:S(2)}) async-start(), calls=%async_computation.9 | async-start | bytes 4866048 | tf_op jit(solution)/shard_map/all_gather | solution.py:285
  12.7 220.9 %all-gather.18.cloned.1.call-start = ((), (), s32[]{:S(2)}) async-start(), calls=%async_computation.10 | async-start | bytes 9732096 | tf_op jit(solution)/shard_map/all_gather | solution.py:285
  58.3 19.9 %copy-start.46 = (f32[768]{0:T(1024)}, f32[768]{0:T(1024)S(1)}, u32[]{:S(2)}) copy-start(f32[768]{0:T(1024)S(1)} %mul.251) | copy-start | bytes 9220
  58.3 19.8 %copy-start.48 = (f32[768]{0:T(1024)}, f32[768]{0:T(1024)S(1)}, u32[]{:S(2)}) copy-start(f32[768]{0:T(1024)S(1)} %add.156) | copy-start | bytes 9220
  64.5 3.9 copy-start.2
  64.6 3.9 copy-start.31
  64.7 13.4 %copy-start.51 = (f32[392]{0:T(512)}, f32[392]{0:T(512)S(1)}, u32[]{:S(2)}) copy-start(f32[392]{0:T(512)S(1)} %div.57) | copy-start | bytes 4708
  66.8 16.2 %copy-start.33 = (f32[2,196]{0,1:T(8,128)}, f32[2,196]{0,1:T(8,128)S(1)}, u32[]{:S(2)}) copy-start(f32[2,196]{0,1:T(8,128)S(1)} %add_rsqrt_fusion) | copy-start | bytes 4708
  67.0 16.0 %copy-start.53 = (f32[392]{0:T(512)}, f32[392]{0:T(512)S(1)}, u32[]{:S(2)}) copy-start(f32[392]{0:T(512)S(1)} %rsqrt.29) | copy-start | bytes 4708
  96.4 5.5 copy-start.18
  104.0 4.4 copy-start.35
  108.4 2.2 copy-start.1
  108.4 2.2 copy-start.44
  119.5 20.3 %all-to-all-start = ((bf16[8,2,25,768]{3,1,2,0:T(2,128)(2,1)}), bf16[8,2,25,768]{3,1,2,0:T(2,128)(2,1)S(1)}, u32[]{:S(2)}, u32[]{:S(2)}) async-start(bf16[8,2,25,768]{3,1,2,0:T(2,128)(2,1)} %bitcast.398), calls=%async_computation | async-start | bytes 1228800 | tf_op jit(solution)/shard_map/all_to_all | solution.py:271
  143.0 12.2 %copy-start.38 = (bf16[16,25,768]{2,0,1:T(8,128)(2,1)}, bf16[16,25,768]{2,0,1:T(8,128)(2,1)S(1)}, u32[]{:S(2)}) copy-start(bf16[16,25,768]{2,0,1:T(8,128)(2,1)S(1)} %reshape.583) | copy-start | bytes 1843204
  165.3 12.1 %copy-start.29 = (bf16[2,25,16,1,6,64]{5,4,3,2,1,0:T(8,128)(2,1)}, bf16[2,25,16,1,6,64]{5,4,3,2,1,0:T(8,128)(2,1)S(1)}, u32[]{:S(2)}) copy-start(bf16[2,25,16,1,6,64]{5,4,3,2,1,0:T(8,128)(2,1)S(1)} %get-tuple-element.152) | copy-start | bytes 1843204
  183.2 3.0 copy-start.39
  189.4 13.9 %all-to-all-start.1 = ((bf16[8,2,25,768]{3,1,2,0:T(2,128)(2,1)}), bf16[8,2,25,768]{3,1,2,0:T(2,128)(2,1)S(1)}, u32[]{:S(2)}, u32[]{:S(2)}) async-start(bf16[8,2,25,768]{3,1,2,0:T(2,128)(2,1)} %copy.315), calls=%async_computation.1 | async-start | bytes 1228800 | tf_op jit(solution)/shard_map/all_to_all | solution.py:279
  233.6 15.7 %copy-start.25 = (f32[392,768]{1,0:T(8,128)S(1)}, f32[392,768]{1,0:T(8,128)}, u32[]{:S(2)}) copy-start(f32[392,768]{1,0:T(8,128)} %reshape.594) | copy-start | bytes 3612676
  233.6 15.7 %copy-start.66 = (bf16[1536,3072]{1,0:T(8,128)(2,1)S(1)}, bf16[1536,3072]{1,0:T(8,128)(2,1)}, u32[]{:S(2)}) copy-start(bf16[1536,3072]{1,0:T(8,128)(2,1)} %all-gather.18.cloned.1.call-done) | copy-start | bytes 28311556
  249.3 12.6 %copy-start.68 = (bf16[2,392,1536]{2,1,0:T(8,128)(2,1)}, bf16[2,392,1536]{2,1,0:T(8,128)(2,1)S(1)}, u32[]{:S(2)}) copy-start(bf16[2,392,1536]{2,1,0:T(8,128)(2,1)S(1)} %get-tuple-element.144) | copy-start | bytes 7225348
  249.3 6.7 %copy-start.10 = (f32[392,768]{1,0:T(8,128)S(1)}, f32[392,768]{1,0:T(8,128)}, u32[]{:S(2)}) copy-start(f32[392,768]{1,0:T(8,128)} %copy-done.9) | copy-start | bytes 3612676
  280.5 13.3 %all-to-all-start.2 = ((bf16[8,2,25,768]{3,1,2,0:T(2,128)(2,1)}), bf16[8,2,25,768]{3,1,2,0:T(2,128)(2,1)S(1)}, u32[]{:S(2)}, u32[]{:S(2)}) async-start(bf16[8,2,25,768]{3,1,2,0:T(2,128)(2,1)} %bitcast.397), calls=%async_computation.2 | async-start | bytes 1228800 | tf_op jit(solution)/shard_map/all_to_all | solution.py:271
  297.1 6.1 %copy-start.41 = (bf16[16,25,768]{2,0,1:T(8,128)(2,1)}, bf16[16,25,768]{2,0,1:T(8,128)(2,1)S(1)}, u32[]{:S(2)}) copy-start(bf16[16,25,768]{2,0,1:T(8,128)(2,1)S(1)} %reshape.597) | copy-start | bytes 1843204
  303.1 3.8 copy-start.17
  303.1 3.9 copy-start.30
  307.8 5.9 %copy-start.24 = (bf16[2,25,6,64,16]{3,4,2,1,0:T(8,128)(2,1)}, bf16[2,25,6,64,16]{3,4,2,1,0:T(8,128)(2,1)S(1)}, u32[]{:S(2)}) copy-start(bf16[2,25,6,64,16]{3,4,2,1,0:T(8,128)(2,1)S(1)} %fusion.104) | copy-start | bytes 1843204
  307.8 1.9 copy-start.15
  333.4 13.3 %all-to-all-start.3 = ((bf16[8,2,25,768]{3,1,2,0:T(2,128)(2,1)}), bf16[8,2,25,768]{3,1,2,0:T(2,128)(2,1)S(1)}, u32[]{:S(2)}, u32[]{:S(2)}) async-start(bf16[8,2,25,768]{3,1,2,0:T(2,128)(2,1)} %copy.326), calls=%async_computation.3 | async-start | bytes 1228800 | tf_op jit(solution)/shard_map/all_to_all | solution.py:279
  337.0 201.4 %all-gather.10.cloned.1.call-start = ((), (), s32[]{:S(2)}) async-start(), calls=%async_computation.5 | async-start | bytes 1843200 | tf_op jit(solution)/shard_map/all_gather | solution.py:484
  346.1 196.2 %all-gather.12.cloned.1.call-start = ((), (), s32[]{:S(2)}) async-start(), calls=%async_computation.6 | async-start | bytes 1843200 | tf_op jit(solution)/shard_map/all_gather | solution.py:484
  354.3 1.9 copy-start.5
  354.3 2.0 copy-start.11
  357.8 10.1 %slice-start = ((s8[4915200]{0:T(1024)(128)(4,1)}), s8[720896]{0:T(1024)(128)(4,1)S(1)}, s32[]{:S(2)}) async-start(s8[4915200]{0:T(1024)(128)(4,1)} %bitcast.385), calls=%async_computation.11 | async-start | bytes 1441792
  359.8 4.4 copy-start.45
  364.3 3.9 slice-start.1
  364.3 4.1 copy-start.36
  364.3 4.3 copy-start.37
  368.6 3.9 copy-start.27
  377.3 6.6 %copy-start.47 = (f32[768]{0:T(1024)S(1)}, f32[768]{0:T(1024)}, u32[]{:S(2)}) copy-start(f32[768]{0:T(1024)} %copy-done.46) | copy-start | bytes 9220
  377.3 6.6 %copy-start.52 = (f32[392]{0:T(512)S(1)}, f32[392]{0:T(512)}, u32[]{:S(2)}) copy-start(f32[392]{0:T(512)} %copy-done.51) | copy-start | bytes 4708
  377.3 6.6 %copy-start.54 = (f32[392]{0:T(512)S(1)}, f32[392]{0:T(512)}, u32[]{:S(2)}) copy-start(f32[392]{0:T(512)} %copy-done.53) | copy-start | bytes 4708
  383.8 5.3 copy-start.7
  390.6 187.3 %reduce-scatter.2.cloned.1.call-start = ((), (), s32[]{:S(2)}) async-start(), calls=%async_computation.7 | async-start | bytes 9732096 | tf_op jit(solution)/shard_map/reduce_scatter | solution.py:452
  404.8 2.7 copy-start.40
  421.6 6.0 %copy-start.8 = (f32[392,768]{1,0:T(8,128)S(1)}, f32[392,768]{1,0:T(8,128)}, u32[]{:S(2)}) copy-start(f32[392,768]{1,0:T(8,128)} %copy-done.6) | copy-start | bytes 3612676
  421.6 6.1 %copy-start.26 = (bf16[2,392,384]{1,2,0:T(8,128)(2,1)S(1)}, bf16[2,392,384]{1,2,0:T(8,128)(2,1)}, u32[]{:S(2)}) copy-start(bf16[2,392,384]{1,2,0:T(8,128)(2,1)} %reshape.579) | copy-start | bytes 1806340
  432.9 9.6 %copy-start.22 = (bf16[2,2,6,64,196]{4,3,2,1,0:T(8,128)(2,1)S(1)}, bf16[2,2,6,64,196]{4,3,2,1,0:T(8,128)(2,1)}, u32[]{:S(2)}) copy-start(bf16[2,2,6,64,196]{4,3,2,1,0:T(8,128)(2,1)} %copy-done.21) | copy-start | bytes 1806340
  449.4 4.1 copy-start
  (17 other events, 21.0 us)
Sparse Core Ops, SparseCore 0:
  11.6 66.4 all-gather.13
  81.6 68.7 all-gather.15
  153.9 79.6 all-gather.17
  346.2 23.0 all-gather.9
  390.7 22.6 all-gather.11
  419.1 158.6 reduce-scatter.1
